TPU v7x, 256 devices: a whole 4x4x8 slice. The times are simulated.
256 devices in a mesh: gx: 4 (over x), gy: 16 (over z, core), gz: 4 (over y).
Axes of the slice: x: 4, y: 4, z: 8, core: 2. Of those that a mesh axis runs over, the one named last changes fastest.
Arguments:
- volume: float32 [512, 1024, 512], P('gx', 'gy', 'gz'), may hold values from -6 to 6
Outputs:
- prefix: float32 [512, 1024, 512], P('gx', 'gy', 'gz')
- box_sum: float32 [512, 1024, 512], P('gx', 'gy', 'gz')
All inputs are finite; a program needn't handle non-finite values.
Results may differ from a plain program's by a relative error of at most 0.00055.
Values sent between devices are 32-bit elements; how exact they have to be, the bound alone decides.
No kernel may reach another device: no remote copies, remote signals or barrier semaphores. Data moves between devices by JAX's collectives and lax.ppermute only.
A program may use at most 128 MiB of HBM per device.

v0:
```python
import functools
import math

import jax
import jax.numpy as jnp
from jax import lax
from jax.experimental import pallas as pl
from jax.experimental.pallas import tpu as pltpu
from jax.sharding import PartitionSpec as P


F32, BF16 = jnp.float32, jnp.bfloat16
MIB = 1 << 20


def iota(shape, dim):
    return lax.broadcasted_iota(jnp.int32, shape, dim)


def split(v):
    high = v.astype(BF16)
    return high, (v - high.astype(F32)).astype(BF16)


def ones_where(keep):
    return jnp.where(keep, 1.0, 0.0).astype(BF16)


def times(v, ones):
    high, low = split(v)
    dot = functools.partial(jnp.dot, preferred_element_type=F32)
    return dot(high, ones) + dot(low, ones)


def times_left(ones, v):
    high, low = split(v)
    dot = functools.partial(jnp.dot, preferred_element_type=F32)
    return dot(ones, high) + dot(ones, low)


def upper(n):
    return ones_where(iota((n, n), 0) <= iota((n, n), 1))


def lower(n):
    return ones_where(iota((n, n), 1) <= iota((n, n), 0))


def scan_rows(v):
    dim, n = v.ndim - 2, v.shape[-2]
    step = 1
    while step < n:
        if step < 8:
            moved = jnp.where(iota(v.shape, dim) >= step, pltpu.roll(v, step, dim), 0.0)
        else:
            kept = lax.slice_in_dim(v, 0, n - step, axis=dim)
            moved = jnp.concatenate([jnp.zeros_like(lax.slice_in_dim(v, 0, step, axis=dim)), kept], axis=dim)
        v = v + moved
        step *= 2
    return v


def five_rows(v):
    n = v.shape[0]
    two = v[: n - 1] + v[1:]
    four = two[: n - 3] + two[2:]
    return four[: n - 4] + v[4:]


def cost(flops, moved):
    return pl.CostEstimate(flops=flops, bytes_accessed=moved, transcendentals=0)


def call(body, out, grid=None, ins=None, outs=None, scratch=(), flops=1 << 20, moved=1 << 20, vmem=24):
    shapes = [jax.ShapeDtypeStruct(s, F32) for s in out]
    kw = {}
    if grid is not None:
        kw = dict(grid=grid, in_specs=ins, out_specs=outs)
    return pl.pallas_call(
        body,
        out_shape=shapes,
        scratch_shapes=list(scratch),
        compiler_params=pltpu.CompilerParams(vmem_limit_bytes=vmem * MIB),
        cost_estimate=cost(flops, moved),
        **kw,
    )


def whole(shape):
    return pl.BlockSpec(shape, lambda *_: (0,) * len(shape))


def totals_body(pieces, v_ref, held_ref, rz_ref, rx_ref, ry_ref, sems):
    nx, ny, nz = held_ref.shape
    n = nx // pieces
    copies = [
        pltpu.make_async_copy(v_ref.at[pl.ds(k * n, n)], held_ref.at[pl.ds(k * n, n)], sems.at[k]) for k in range(pieces)
    ]
    for copy in copies:
        copy.start()
    lane = iota((ny, nx), 1)

    def group(i, carry):
        rz, rx = carry
        rows = []
        for j in range(8):
            v = held_ref[i * 8 + j]
            rx = rx + v
            rows.append(jnp.sum(v, axis=0, keepdims=True))
            rz = jnp.where(lane == i * 8 + j, jnp.sum(v, axis=1, keepdims=True), rz)
        ry_ref[pl.ds(pl.multiple_of(i * 8, 8), 8), :] = jnp.concatenate(rows, axis=0)
        return rz, rx

    carry = jnp.zeros((ny, nx), F32), jnp.zeros((ny, nz), F32)
    for k, copy in enumerate(copies):
        copy.wait()
        carry = lax.fori_loop(k * n // 8, (k + 1) * n // 8, group, carry)
    rz_ref[...], rx_ref[...] = carry


def totals(v):
    nx, ny, nz = v.shape
    pieces = 4
    out = [v.shape, (ny, nx), (ny, nz), (nx, nz)]
    return pl.pallas_call(
        functools.partial(totals_body, pieces),
        out_shape=[jax.ShapeDtypeStruct(s, F32) for s in out],
        in_specs=[pl.BlockSpec(memory_space=pltpu.HBM)],
        out_specs=[pl.BlockSpec(memory_space=pltpu.VMEM)] * 4,
        scratch_shapes=[pltpu.SemaphoreType.DMA((pieces,))],
        compiler_params=pltpu.CompilerParams(vmem_limit_bytes=24 * MIB),
        cost_estimate=cost(6 << 20, 8 << 20),
    )(v)


def lower_sum(own, parts):
    total = jnp.where(own >= 1, parts[0][...], 0.0)
    for d in range(1, len(parts)):
        total = total + jnp.where(own >= d + 1, parts[d][...], 0.0)
    return total


def after_z_body(r1, r2, r3, rx_ref, cz_ref, out_ref):
    cz = lower_sum(lax.axis_index("gz"), (r1, r2, r3))
    cz_ref[...] = cz
    rx = rx_ref[...]
    out_ref[...] = rx + jnp.where(iota(rx.shape, 1) == 0, jnp.sum(cz, axis=1, keepdims=True), 0.0)


def after_x_body(r1, r2, r3, cz_ref, ry_ref, cx_ref, out_ref):
    cx = lower_sum(lax.axis_index("gx"), (r1, r2, r3))
    cx_ref[...] = cx
    ry = ry_ref[...]
    n = ry.shape[0]
    row = jnp.sum(cz_ref[...], axis=0, keepdims=True)
    column = jnp.sum(jnp.where(iota((n, n), 0) == iota((n, n), 1), row, 0.0), axis=1, keepdims=True)
    ry = ry + jnp.where(iota(ry.shape, 1) == 0, column, 0.0)
    out_ref[...] = ry + jnp.where(iota(ry.shape, 0) == 0, jnp.sum(cx, axis=0, keepdims=True), 0.0)


def pair_body(mine_ref, other_ref, out_ref):
    core = lax.rem(lax.axis_index("gy"), 2)
    n = out_ref.shape[0]
    both = mine_ref[...] + other_ref[...]
    out_ref[...] = jnp.where(core == 0, both[:n], both[n:])


def round_body(by, from_ref, own_ref, *refs):
    chip = lax.div(lax.axis_index("gy"), 2)
    got = jnp.where(chip >= by, from_ref[...], 0.0)
    low_refs, (low_out, *own_out) = refs[:-2] if by < 4 else refs[:-1], refs[-2:] if by < 4 else refs[-1:]
    low_out[...] = got + low_refs[0][...] if low_refs else got
    for ref in own_out:
        ref[...] = got + own_ref[...]


def local_body(nb, v_ref, cz_ref, cx_ref, out_ref, acc):
    i = pl.program_id(0)
    ny, nz = acc.shape
    up = upper(nz)

    @pl.when(i == 0)
    def _():
        acc[...] = scan_rows(times(cx_ref[...], up))

    lane = iota((ny, nz), 1)
    cz = cz_ref[...]
    rows = []
    for j in range(nb):
        x = i * nb + j
        rows.append(v_ref[j] + jnp.where(lane == 0, pltpu.roll(cz, lax.rem(nz - x, nz), 1), 0.0))
    along = times(jnp.concatenate(rows, axis=0), up).reshape(nb, ny, nz)
    total = acc[...]
    for j in range(nb):
        total = total + scan_rows(along[j])
        out_ref[j] = total
    acc[...] = total


def local(v, cz, cx):
    nx, ny, nz = v.shape
    nb = 32
    return call(
        functools.partial(local_body, nb),
        [v.shape],
        grid=(nx // nb,),
        ins=[pl.BlockSpec((nb, ny, nz), lambda i: (i, 0, 0)), whole(cz.shape), whole(cx.shape)],
        outs=[pl.BlockSpec((nb, ny, nz), lambda i: (i, 0, 0))],
        scratch=[pltpu.VMEM((ny, nz), F32)],
        flops=1 << 29,
        moved=8 << 20,
    )(v, cz, cx)[0]


def last_body(nb, scale, s_ref, half_ref, other_half_ref, partner_ref, out_ref, gy):
    i = pl.program_id(0)

    @pl.when(i == 0)
    def _():
        core = lax.rem(lax.axis_index("gy"), 2)
        mine, other = half_ref[...], other_half_ref[...]
        cy = jnp.concatenate([jnp.where(core == 0, mine, other), jnp.where(core == 0, other, mine)], axis=0)
        cy = cy + jnp.where(core == 1, partner_ref[...], 0.0)
        gy[...] = times_left(lower(cy.shape[0]), times(cy, upper(cy.shape[1])))

    rows = gy[pl.ds(pl.multiple_of(i * nb, nb), nb), :]
    for j in range(nb):
        out_ref[j] = (s_ref[j] + rows[j : j + 1]) * scale


def last(s, half, other_half, partner, scale):
    nx, ny, nz = s.shape
    nb = 32
    return call(
        functools.partial(last_body, nb, scale),
        [s.shape],
        grid=(nx // nb,),
        ins=[pl.BlockSpec((nb, ny, nz), lambda i: (i, 0, 0)), whole(half.shape), whole(half.shape), whole(partner.shape)],
        outs=[pl.BlockSpec((nb, ny, nz), lambda i: (i, 0, 0))],
        scratch=[pltpu.VMEM((nx, nz), F32)],
        flops=1 << 24,
        moved=8 << 20,
    )(s, half, other_half, partner)[0]


def strips_body(sizes, first_ref, last_ref, lo_a, lo_b, hi_a, hi_b, up_ref, down_ref):
    own = lax.axis_index("gx")
    has_lo, has_hi = own > 0, own < sizes["gx"] - 1
    for v_ref, lo_ref, hi_ref, out_ref, at in ((first_ref, lo_a, hi_a, down_ref, 0), (last_ref, lo_b, hi_b, up_ref, 6)):
        for layer in range(2):
            lo = jnp.where(has_lo, lo_ref[:, at + layer, :], 0.0)
            hi = jnp.where(has_hi, hi_ref[:, at + layer, :], 0.0)
            out_ref[layer] = five_rows(jnp.concatenate([lo, v_ref[:, at + layer, :], hi], axis=0))


def strips(v, x_lo, x_hi, sizes):
    nx, ny, nz = v.shape
    end = ny // 8 - 1
    at_first, at_last = lambda i: (0, 0, 0), lambda i: (0, end, 0)
    return call(
        functools.partial(strips_body, sizes),
        [(2, nx, nz), (2, nx, nz)],
        grid=(1,),
        ins=[
            pl.BlockSpec((nx, 8, nz), at_first),
            pl.BlockSpec((nx, 8, nz), at_last),
            pl.BlockSpec((2, 8, nz), at_first),
            pl.BlockSpec((2, 8, nz), at_last),
            pl.BlockSpec((2, 8, nz), at_first),
            pl.BlockSpec((2, 8, nz), at_last),
        ],
        outs=[whole((2, nx, nz)), whole((2, nx, nz))],
        flops=1 << 22,
        moved=2 << 20,
    )(v, v, x_lo, x_lo, x_hi, x_hi)


def box_xy_body(nb, sizes, v_ref, x_lo, x_hi, y_lo, y_hi, out_ref, up_ref, down_ref):
    i = pl.program_id(0)
    steps = pl.num_programs(0)
    gx, gy = lax.axis_index("gx"), lax.axis_index("gy")
    ny, nz = v_ref.shape[1:]
    base = pl.multiple_of(i * nb, nb)
    group = lax.div(i * nb * 2, nz)

    def run(first, final):
        def row(j):
            if first and j < 0:
                return jnp.where(gx > 0, x_lo[j + 2], 0.0)
            if final and j >= nb:
                return jnp.where(gx < sizes["gx"] - 1, x_hi[j - nb], 0.0)
            return v_ref[base + j]

        lane = iota((ny, nz), 1)
        lows = [jnp.where(gy > 0, y_lo[l, pl.ds(base, nb), :], 0.0) for l in range(2)]
        highs = [jnp.where(gy < sizes["gy"] - 1, y_hi[l, pl.ds(base, nb), :], 0.0) for l in range(2)]
        up = jnp.zeros((ny, nz), F32)
        down = jnp.zeros((ny, nz), F32)
        twos = {j: row(j) + row(j + 1) for j in range(-2, nb + 1)}
        for j in range(nb):
            along = twos[j - 2] + twos[j] + row(j + 2)
            ext = jnp.concatenate(
                [lows[0][j : j + 1], lows[1][j : j + 1], along, highs[0][j : j + 1], highs[1][j : j + 1]], axis=0
            )
            box = five_rows(ext)
            out_ref[j] = box
            at = lax.rem(base + j, nz // 2) * 2
            here = lax.div(lane, 2) * 2 == at
            up = jnp.where(here, pltpu.roll(box, lax.rem(at + 2, nz), 1), up)
            down = jnp.where(here, pltpu.roll(box, at, 1), down)
        at0 = lax.rem(base, nz // 2) * 2
        mine = jnp.logical_and(lane >= at0, lane < at0 + 2 * nb)
        up_ref[group] = jnp.where(mine, up, up_ref[group])
        down_ref[group] = jnp.where(mine, down, down_ref[group])

    pl.when(i == 0)(lambda: run(True, False))
    pl.when(i == steps - 1)(lambda: run(False, True))
    pl.when(jnp.logical_and(i > 0, i < steps - 1))(lambda: run(False, False))


def box_xy(v, x_lo, x_hi, y_lo, y_hi, sizes):
    nx, ny, nz = v.shape
    nb = 32
    packed = (2 * nx // nz, ny, nz)
    return call(
        functools.partial(box_xy_body, nb, sizes),
        [v.shape, packed, packed],
        grid=(nx // nb,),
        ins=[whole(v.shape), whole(x_lo.shape), whole(x_hi.shape), whole(y_lo.shape), whole(y_hi.shape)],
        outs=[pl.BlockSpec((nb, ny, nz), lambda i: (i, 0, 0)), whole(packed), whole(packed)],
        flops=1 << 26,
        moved=8 << 20,
    )(v, x_lo, x_hi, y_lo, y_hi)


def box_z_body(nb, sizes, scale, w_ref, lo_ref, hi_ref, out_ref, lo, hi):
    i = pl.program_id(0)
    gz = lax.axis_index("gz")
    nz = w_ref.shape[2]
    ny = w_ref.shape[1]

    @pl.when(i == 0)
    def _():
        for g in range(lo.shape[0]):
            even = lax.rem(iota((ny, nz), 1), 2) == 0
            a, b = lo_ref[g], hi_ref[g]
            a = a + jnp.where(even, pltpu.roll(a, nz - 1, 1), 0.0)
            b = b + jnp.where(even, 0.0, pltpu.roll(b, 1, 1))
            lo[g] = jnp.where(gz > 0, a, 0.0)
            hi[g] = jnp.where(gz < sizes["gz"] - 1, b, 0.0)

    away = iota((nz, nz), 0) - iota((nz, nz), 1)
    band = ones_where(jnp.logical_and(away <= 2, away >= -2))
    along = times(w_ref[...].reshape(nb * ny, nz), band).reshape(nb, ny, nz)
    lane = iota((ny, nz), 1)
    group = lax.div(i * nb * 2, nz)
    a, b = lo[group], hi[group]
    for j in range(nb):
        at = lax.rem(i * nb + j, nz // 2) * 2
        left = pltpu.roll(a, lax.rem(nz - at, nz), 1)
        right = pltpu.roll(b, lax.rem(2 * nz - 2 - at, nz), 1)
        side = jnp.where(lane < 2, left, jnp.where(lane >= nz - 2, right, 0.0))
        out_ref[j] = (along[j] + side) * scale


def box_z(w, lo, hi, sizes, scale):
    nx, ny, nz = w.shape
    nb = 32
    return call(
        functools.partial(box_z_body, nb, sizes, scale),
        [w.shape],
        grid=(nx // nb,),
        ins=[pl.BlockSpec((nb, ny, nz), lambda i: (i, 0, 0)), whole(lo.shape), whole(hi.shape)],
        outs=[pl.BlockSpec((nb, ny, nz), lambda i: (i, 0, 0))],
        scratch=[pltpu.VMEM(lo.shape, F32), pltpu.VMEM(lo.shape, F32)],
        flops=1 << 29,
        moved=8 << 20,
    )(w, lo, hi)[0]


def shift(v, axis, by):
    n = lax.axis_size(axis)
    return lax.ppermute(v, axis, [(i, (i + by) % n) for i in range(n)])


def partner(v):
    return lax.ppermute(v, "gy", [(i, i ^ 1) for i in range(lax.axis_size("gy"))])


def per_device(v):
    nx, ny, nz = v.shape
    sizes = {a: lax.axis_size(a) for a in ("gx", "gy", "gz")}
    cells = nx * ny * nz * sizes["gx"] * sizes["gy"] * sizes["gz"]

    held, rz, rx, ry = totals(v)

    from_z = [shift(rz, "gz", d) for d in (1, 2, 3)]
    x_lo, x_hi = shift(held[nx - 2 :], "gx", 1), shift(held[:2], "gx", -1)
    cz, rx = call(after_z_body, [rz.shape, rx.shape])(*from_z, rx)

    from_x = [shift(rx, "gx", d) for d in (1, 2, 3)]
    up, down = strips(held, x_lo, x_hi, sizes)
    y_lo, y_hi = shift(up, "gy", 1), shift(down, "gy", -1)
    cx, ry = call(after_x_body, [rx.shape, ry.shape])(*from_x, cz, ry)

    other = partner(ry)
    shape = (nx // 2, nz)
    (half,) = call(pair_body, [shape])(ry, other)
    got = shift(half, "gy", 2)
    w, up, down = box_xy(held, x_lo, x_hi, y_lo, y_hi, sizes)
    low, half = call(functools.partial(round_body, 1), [shape] * 2)(got, half)
    got = shift(half, "gy", 4)
    z_lo, z_hi = shift(up, "gz", 1), shift(down, "gz", -1)
    s = local(held, cz, cx)
    low, half = call(functools.partial(round_body, 2), [shape] * 2)(got, half, low)
    got = shift(half, "gy", 8)
    box_sum = box_z(w, z_lo, z_hi, sizes, 1.0 / math.sqrt(125.0))
    (low,) = call(functools.partial(round_body, 4), [shape])(got, half, low)
    other_low = partner(low)
    prefix = last(s, low, other_low, other, 1.0 / math.sqrt(cells))
    return (prefix, box_sum)


def solution(mesh):
    return jax.shard_map(
        per_device,
        mesh=mesh,
        in_specs=(P("gx", "gy", "gz"),),
        out_specs=(P("gx", "gy", "gz"), P("gx", "gy", "gz")),
        check_vma=False,
    )
```

profile of v0, /device:TPU:1, one launch (start us, length us, event | category | flops | bytes accessed | tf_op | source)
XLA Modules:
  0.0 62.9 jit_solution(10424261766026721651)
XLA Ops:
  0.6 0.0 copy-start
  0.6 2.2 %copy-done = f32[128,64,128]{2,1,0:T(8,128)S(1)} copy-done((f32[128,64,128]{2,1,0:T(8,128)S(1)}, f32[128,64,128]{2,1,0:T(8,128)}, u32[]{:S(2)}) %copy-start) | copy-done | bytes 4194328
  2.8 2.6 %shard_map.30 = (f32[128,64,128]{2,1,0:T(8,128)S(1)}, f32[64,128]{1,0:T(8,128)S(1)}, f32[64,128]{1,0:T(8,128)S(1)}, f32[128,128]{1,0:T(8,128)S(1)}) custom-call(f32[128,64,128]{2,1,0:T(8,128)S(1)} %copy-done), custom_call_target="tpu_custom_call" | custom-call | flops 6291456 | bytes 8388608 | tf_op jit(solution)/shard_map/pallas_call | solution.py:125
  5.4 2.2 %collective-permute-start = (f32[64,128]{1,0:T(8,128)S(1)}, f32[64,128]{1,0:T(8,128)S(1)}, u32[]{:S(2)}, u32[]{:S(2)}) collective-permute-start(f32[64,128]{1,0:T(8,128)S(1)} %get-tuple-element.20), channel_id=1, source_target_pairs={{0,1},{1,2},{2,3},{3,0},{4,5},{5,6},{6,7},{7,4},{8,9},{9,10},{10,1... | collective-permute-start | bytes 98312 | tf_op jit(solution)/shard_map/ppermute | solution.py:383
  7.6 2.6 %collective-permute-start.1 = (f32[64,128]{1,0:T(8,128)S(1)}, f32[64,128]{1,0:T(8,128)S(1)}, u32[]{:S(2)}, u32[]{:S(2)}) collective-permute-start(f32[64,128]{1,0:T(8,128)S(1)} %get-tuple-element.20), channel_id=1, source_target_pairs={{0,2},{1,3},{2,0},{3,1},{4,6},{5,7},{6,4},{7,5},{8,10},{9,11},{10,... | collective-permute-start | bytes 98312 | tf_op jit(solution)/shard_map/ppermute | solution.py:383
  10.2 1.1 %collective-permute-start.2 = (f32[64,128]{1,0:T(8,128)S(1)}, f32[64,128]{1,0:T(8,128)S(1)}, u32[]{:S(2)}, u32[]{:S(2)}) collective-permute-start(f32[64,128]{1,0:T(8,128)S(1)} %get-tuple-element.20), channel_id=1, source_target_pairs={{0,3},{1,0},{2,1},{3,2},{4,7},{5,4},{6,5},{7,6},{8,11},{9,8},{10,9... | collective-permute-start | bytes 98312 | tf_op jit(solution)/shard_map/ppermute | solution.py:383
  11.3 1.3 %collective-permute-start.11 = (f32[2,64,128]{2,1,0:T(8,128)S(1)}, f32[2,64,128]{2,1,0:T(8,128)S(1)}, u32[]{:S(2)}, u32[]{:S(2)}) collective-permute-start(f32[2,64,128]{2,1,0:T(8,128)S(1)} %get-tuple-element.37), channel_id=1, source_target_pairs={{0,64},{64,128},{128,192},{192,0},{1,65},{65,129},{129,193},{193,1... | collective-permute-start | bytes 196616 | tf_op jit(solution)/shard_map/ppermute | solution.py:383
  12.6 1.5 %collective-permute-start.12 = (f32[2,64,128]{2,1,0:T(8,128)S(1)}, f32[2,64,128]{2,1,0:T(8,128)S(1)}, u32[]{:S(2)}, u32[]{:S(2)}) collective-permute-start(f32[2,64,128]{2,1,0:T(8,128)S(1)} %get-tuple-element.36), channel_id=1, source_target_pairs={{0,192},{64,0},{128,64},{192,128},{1,193},{65,1},{129,65},{193,129... | collective-permute-start | bytes 196616 | tf_op jit(solution)/shard_map/ppermute | solution.py:383
  14.1 0.0 collective-permute-done.r1
  14.1 0.0 collective-permute-done.1.r2
  14.1 0.0 collective-permute-done.2.r3
  14.1 0.1 shard_map.31
  14.2 0.4 collective-permute-start.3
  14.6 2.5 %collective-permute-start.4 = (f32[64,128]{1,0:T(8,128)S(1)}, f32[64,128]{1,0:T(8,128)S(1)}, u32[]{:S(2)}, u32[]{:S(2)}) collective-permute-start(f32[64,128]{1,0:T(8,128)S(1)} %get-tuple-element.23), channel_id=1, source_target_pairs={{0,128},{64,192},{128,0},{192,64},{1,129},{65,193},{129,1},{193,65... | collective-permute-start | bytes 98312 | tf_op jit(solution)/shard_map/ppermute | solution.py:383
  17.1 1.2 %collective-permute-start.5 = (f32[64,128]{1,0:T(8,128)S(1)}, f32[64,128]{1,0:T(8,128)S(1)}, u32[]{:S(2)}, u32[]{:S(2)}) collective-permute-start(f32[64,128]{1,0:T(8,128)S(1)} %get-tuple-element.23), channel_id=1, source_target_pairs={{0,192},{64,0},{128,64},{192,128},{1,193},{65,1},{129,65},{193,129... | collective-permute-start | bytes 98312 | tf_op jit(solution)/shard_map/ppermute | solution.py:383
  18.2 0.0 collective-permute-done.3.r1
  18.2 1.2 %collective-permute-done.4.r2 = f32[64,128]{1,0:T(8,128)S(1)} collective-permute-done((f32[64,128]{1,0:T(8,128)S(1)}, f32[64,128]{1,0:T(8,128)S(1)}, u32[]{:S(2)}, u32[]{:S(2)}) %collective-permute-start.4) | collective-permute-done | bytes 32800 | tf_op jit(solution)/shard_map/ppermute | solution.py:383
  19.4 0.4 collective-permute-done.5.r3
  19.8 0.1 shard_map.32
  19.9 3.9 %collective-permute-start.6 = (f32[128,128]{1,0:T(8,128)S(1)}, f32[128,128]{1,0:T(8,128)S(1)}, u32[]{:S(2)}, u32[]{:S(2)}) collective-permute-start(f32[128,128]{1,0:T(8,128)S(1)} %get-tuple-element.26.mine_ref), channel_id=1, source_target_pairs={{0,4},{4,0},{8,12},{12,8},{16,20},{20,16},{24,28},{28,24},{32,36},... | collective-permute-start | bytes 196616 | tf_op jit(solution)/shard_map/ppermute | solution.py:387
  23.8 0.0 collective-permute-done.11.lo_a.lo_b.x_lo
  23.8 0.0 collective-permute-done.12.hi_a.hi_b.x_hi
  23.8 0.3 shard_map.39
  24.2 1.6 %collective-permute-start.13 = (f32[2,128,128]{2,1,0:T(8,128)S(1)}, f32[2,128,128]{2,1,0:T(8,128)S(1)}, u32[]{:S(2)}, u32[]{:S(2)}) collective-permute-start(f32[2,128,128]{2,1,0:T(8,128)S(1)} %get-tuple-element.31), channel_id=1, source_target_pairs={{0,4},{4,8},{8,12},{12,16},{16,20},{20,24},{24,28},{28,32},{32,36}... | collective-permute-start | bytes 393224 | tf_op jit(solution)/shard_map/ppermute | solution.py:383
  25.7 0.0 collective-permute-start.14
  25.7 0.0 collective-permute-done.6.other_ref.partner_ref
  25.8 1.7 %collective-permute-start.7 = (f32[64,128]{1,0:T(8,128)S(1)}, f32[64,128]{1,0:T(8,128)S(1)}, u32[]{:S(2)}, u32[]{:S(2)}) collective-permute-start(f32[64,128]{1,0:T(8,128)S(1)} %shard_map.34.own_ref), channel_id=1, source_target_pairs={{0,8},{4,12},{8,16},{12,20},{16,24},{20,28},{24,32},{28,36},{32,40... | collective-permute-start | bytes 98312 | tf_op jit(solution)/shard_map/ppermute | solution.py:383
  27.5 5.0 %collective-permute-done.7.from_ref = f32[64,128]{1,0:T(8,128)S(1)} collective-permute-done((f32[64,128]{1,0:T(8,128)S(1)}, f32[64,128]{1,0:T(8,128)S(1)}, u32[]{:S(2)}, u32[]{:S(2)}) %collective-permute-start.7) | collective-permute-done | bytes 32800 | tf_op jit(solution)/shard_map/ppermute | solution.py:383
  32.5 0.2 collective-permute-start.8
  32.7 4.9 %collective-permute-done.8.from_ref = f32[64,128]{1,0:T(8,128)S(1)} collective-permute-done((f32[64,128]{1,0:T(8,128)S(1)}, f32[64,128]{1,0:T(8,128)S(1)}, u32[]{:S(2)}, u32[]{:S(2)}) %collective-permute-start.8) | collective-permute-done | bytes 32800 | tf_op jit(solution)/shard_map/ppermute | solution.py:383
  37.7 3.8 %collective-permute-start.9 = (f32[64,128]{1,0:T(8,128)S(1)}, f32[64,128]{1,0:T(8,128)S(1)}, u32[]{:S(2)}, u32[]{:S(2)}) collective-permute-start(f32[64,128]{1,0:T(8,128)S(1)} %get-tuple-element.29.own_ref), channel_id=1, source_target_pairs={{0,32},{4,36},{8,40},{12,44},{16,48},{20,52},{24,56},{28,60},{32,0... | collective-permute-start | bytes 98312 | tf_op jit(solution)/shard_map/ppermute | solution.py:383
  41.5 0.0 collective-permute-done.13.y_lo
  41.5 0.0 collective-permute-done.14.y_hi
  41.5 3.0 %shard_map.40 = (f32[128,64,128]{2,1,0:T(8,128)S(1)}, f32[2,64,128]{2,1,0:T(8,128)S(1)}, f32[2,64,128]{2,1,0:T(8,128)S(1)}) custom-call(f32[128,64,128]{2,1,0:T(8,128)S(1)} %get-tuple-element.19.v_ref.first_ref.last_ref, f32[2,64,128]{2,1,0:T(8,128)S(1)} %collective-permute-done.11.lo_a.lo_b.x_lo, f32[2,64,128]{2,1,0:T(8,128)S(1)} %collective-permute-done.12.hi_a.hi_b.x_hi, ...), custom_call_target="tpu_custom_call" | custom-call | flops 67108864 | bytes 8388608 | tf_op jit(solution)/shard_map/pallas_call | solution.py:325
  44.5 0.3 collective-permute-start.15
  44.7 2.7 %collective-permute-start.16 = (f32[2,64,128]{2,1,0:T(8,128)S(1)}, f32[2,64,128]{2,1,0:T(8,128)S(1)}, u32[]{:S(2)}, u32[]{:S(2)}) collective-permute-start(f32[2,64,128]{2,1,0:T(8,128)S(1)} %get-tuple-element.35), channel_id=1, source_target_pairs={{0,3},{1,0},{2,1},{3,2},{4,7},{5,4},{6,5},{7,6},{8,11},{9,8},{10,9... | collective-permute-start | bytes 196616 | tf_op jit(solution)/shard_map/ppermute | solution.py:383
  47.4 0.0 collective-permute-done.9.from_ref
  47.4 5.2 %collective-permute-start.10 = (f32[64,128]{1,0:T(8,128)S(1)}, f32[64,128]{1,0:T(8,128)S(1)}, u32[]{:S(2)}, u32[]{:S(2)}) collective-permute-start(f32[64,128]{1,0:T(8,128)S(1)} %shard_map.37.half_ref), channel_id=1, source_target_pairs={{0,4},{4,0},{8,12},{12,8},{16,20},{20,16},{24,28},{28,24},{32,36},... | collective-permute-start | bytes 98312 | tf_op jit(solution)/shard_map/ppermute | solution.py:387
  52.7 3.4 %shard_map.33.s_ref = f32[128,64,128]{2,1,0:T(8,128)S(1)} custom-call(f32[128,64,128]{2,1,0:T(8,128)S(1)} %get-tuple-element.19.v_ref.first_ref.last_ref, f32[64,128]{1,0:T(8,128)S(1)} %get-tuple-element.22.cz_ref, f32[64,128]{1,0:T(8,128)S(1)} %get-tuple-element.25.cx_ref), custom_call_target="tpu_custom_call" | custom-call | flops 536870912 | bytes 8388608 | tf_op jit(solution)/shard_map/pallas_call | solution.py:203
  56.1 0.0 collective-permute-done.10.other_half_ref
  56.1 2.8 %shard_map.38 = f32[128,64,128]{2,1,0:T(8,128)} custom-call(f32[128,64,128]{2,1,0:T(8,128)S(1)} %shard_map.33.s_ref, f32[64,128]{1,0:T(8,128)S(1)} %shard_map.37.half_ref, f32[64,128]{1,0:T(8,128)S(1)} %collective-permute-done.10.other_half_ref, f32[128,128]{1,0:T(8,128)S(1)} %collective-permute-done.6.other_ref.partner_ref), custom_call_target="tpu_custom_call" | custom-call | flops 16777216 | bytes 8388608 | tf_op jit(solution)/shard_map/pallas_call | solution.py:234
  58.9 0.0 collective-permute-done.15.lo_ref
  58.9 0.0 collective-permute-done.16.hi_ref
  58.9 4.1 %shard_map.41 = f32[128,64,128]{2,1,0:T(8,128)} custom-call(f32[128,64,128]{2,1,0:T(8,128)S(1)} %get-tuple-element.33.w_ref, f32[2,64,128]{2,1,0:T(8,128)S(1)} %collective-permute-done.15.lo_ref, f32[2,64,128]{2,1,0:T(8,128)S(1)} %collective-permute-done.16.hi_ref), custom_call_target="tpu_custom_call" | custom-call | flops 536870912 | bytes 8388608 | tf_op jit(solution)/shard_map/pallas_call | solution.py:369
  (5 shorter events, 0.0 us)
Async XLA Ops:
  0.6 2.2 %copy-start = (f32[128,64,128]{2,1,0:T(8,128)S(1)}, f32[128,64,128]{2,1,0:T(8,128)}, u32[]{:S(2)}) copy-start(f32[128,64,128]{2,1,0:T(8,128)} %v_ref.1) | copy-start | bytes 12582916
  5.4 8.7 %collective-permute-start = (f32[64,128]{1,0:T(8,128)S(1)}, f32[64,128]{1,0:T(8,128)S(1)}, u32[]{:S(2)}, u32[]{:S(2)}) collective-permute-start(f32[64,128]{1,0:T(8,128)S(1)} %get-tuple-element.20), channel_id=1, source_target_pairs={{0,1},{1,2},{2,3},{3,0},{4,5},{5,6},{6,7},{7,4},{8,9},{9,10},{10,1... | collective-permute-start | bytes 98312 | tf_op jit(solution)/shard_map/ppermute | solution.py:383
  7.6 6.5 %collective-permute-start.1 = (f32[64,128]{1,0:T(8,128)S(1)}, f32[64,128]{1,0:T(8,128)S(1)}, u32[]{:S(2)}, u32[]{:S(2)}) collective-permute-start(f32[64,128]{1,0:T(8,128)S(1)} %get-tuple-element.20), channel_id=1, source_target_pairs={{0,2},{1,3},{2,0},{3,1},{4,6},{5,7},{6,4},{7,5},{8,10},{9,11},{10,... | collective-permute-start | bytes 98312 | tf_op jit(solution)/shard_map/ppermute | solution.py:383
  10.2 3.8 %collective-permute-start.2 = (f32[64,128]{1,0:T(8,128)S(1)}, f32[64,128]{1,0:T(8,128)S(1)}, u32[]{:S(2)}, u32[]{:S(2)}) collective-permute-start(f32[64,128]{1,0:T(8,128)S(1)} %get-tuple-element.20), channel_id=1, source_target_pairs={{0,3},{1,0},{2,1},{3,2},{4,7},{5,4},{6,5},{7,6},{8,11},{9,8},{10,9... | collective-permute-start | bytes 98312 | tf_op jit(solution)/shard_map/ppermute | solution.py:383
  11.3 12.5 %collective-permute-start.11 = (f32[2,64,128]{2,1,0:T(8,128)S(1)}, f32[2,64,128]{2,1,0:T(8,128)S(1)}, u32[]{:S(2)}, u32[]{:S(2)}) collective-permute-start(f32[2,64,128]{2,1,0:T(8,128)S(1)} %get-tuple-element.37), channel_id=1, source_target_pairs={{0,64},{64,128},{128,192},{192,0},{1,65},{65,129},{129,193},{193,1... | collective-permute-start | bytes 196616 | tf_op jit(solution)/shard_map/ppermute | solution.py:383
  12.6 11.2 %collective-permute-start.12 = (f32[2,64,128]{2,1,0:T(8,128)S(1)}, f32[2,64,128]{2,1,0:T(8,128)S(1)}, u32[]{:S(2)}, u32[]{:S(2)}) collective-permute-start(f32[2,64,128]{2,1,0:T(8,128)S(1)} %get-tuple-element.36), channel_id=1, source_target_pairs={{0,192},{64,0},{128,64},{192,128},{1,193},{65,1},{129,65},{193,129... | collective-permute-start | bytes 196616 | tf_op jit(solution)/shard_map/ppermute | solution.py:383
  14.2 4.0 %collective-permute-start.3 = (f32[64,128]{1,0:T(8,128)S(1)}, f32[64,128]{1,0:T(8,128)S(1)}, u32[]{:S(2)}, u32[]{:S(2)}) collective-permute-start(f32[64,128]{1,0:T(8,128)S(1)} %get-tuple-element.23), channel_id=1, source_target_pairs={{0,64},{64,128},{128,192},{192,0},{1,65},{65,129},{129,193},{193,1... | collective-permute-start | bytes 98312 | tf_op jit(solution)/shard_map/ppermute | solution.py:383
  14.6 4.8 %collective-permute-start.4 = (f32[64,128]{1,0:T(8,128)S(1)}, f32[64,128]{1,0:T(8,128)S(1)}, u32[]{:S(2)}, u32[]{:S(2)}) collective-permute-start(f32[64,128]{1,0:T(8,128)S(1)} %get-tuple-element.23), channel_id=1, source_target_pairs={{0,128},{64,192},{128,0},{192,64},{1,129},{65,193},{129,1},{193,65... | collective-permute-start | bytes 98312 | tf_op jit(solution)/shard_map/ppermute | solution.py:383
  17.1 2.8 %collective-permute-start.5 = (f32[64,128]{1,0:T(8,128)S(1)}, f32[64,128]{1,0:T(8,128)S(1)}, u32[]{:S(2)}, u32[]{:S(2)}) collective-permute-start(f32[64,128]{1,0:T(8,128)S(1)} %get-tuple-element.23), channel_id=1, source_target_pairs={{0,192},{64,0},{128,64},{192,128},{1,193},{65,1},{129,65},{193,129... | collective-permute-start | bytes 98312 | tf_op jit(solution)/shard_map/ppermute | solution.py:383
  19.9 5.8 %collective-permute-start.6 = (f32[128,128]{1,0:T(8,128)S(1)}, f32[128,128]{1,0:T(8,128)S(1)}, u32[]{:S(2)}, u32[]{:S(2)}) collective-permute-start(f32[128,128]{1,0:T(8,128)S(1)} %get-tuple-element.26.mine_ref), channel_id=1, source_target_pairs={{0,4},{4,0},{8,12},{12,8},{16,20},{20,16},{24,28},{28,24},{32,36},... | collective-permute-start | bytes 196616 | tf_op jit(solution)/shard_map/ppermute | solution.py:387
  24.2 17.3 %collective-permute-start.13 = (f32[2,128,128]{2,1,0:T(8,128)S(1)}, f32[2,128,128]{2,1,0:T(8,128)S(1)}, u32[]{:S(2)}, u32[]{:S(2)}) collective-permute-start(f32[2,128,128]{2,1,0:T(8,128)S(1)} %get-tuple-element.31), channel_id=1, source_target_pairs={{0,4},{4,8},{8,12},{12,16},{16,20},{20,24},{24,28},{28,32},{32,36}... | collective-permute-start | bytes 393224 | tf_op jit(solution)/shard_map/ppermute | solution.py:383
  25.7 15.7 %collective-permute-start.14 = (f32[2,128,128]{2,1,0:T(8,128)S(1)}, f32[2,128,128]{2,1,0:T(8,128)S(1)}, u32[]{:S(2)}, u32[]{:S(2)}) collective-permute-start(f32[2,128,128]{2,1,0:T(8,128)S(1)} %get-tuple-element.32), channel_id=1, source_target_pairs={{0,60},{4,0},{8,4},{12,8},{16,12},{20,16},{24,20},{28,24},{32,28},... | collective-permute-start | bytes 393224 | tf_op jit(solution)/shard_map/ppermute | solution.py:383
  25.8 6.7 %collective-permute-start.7 = (f32[64,128]{1,0:T(8,128)S(1)}, f32[64,128]{1,0:T(8,128)S(1)}, u32[]{:S(2)}, u32[]{:S(2)}) collective-permute-start(f32[64,128]{1,0:T(8,128)S(1)} %shard_map.34.own_ref), channel_id=1, source_target_pairs={{0,8},{4,12},{8,16},{12,20},{16,24},{20,28},{24,32},{28,36},{32,40... | collective-permute-start | bytes 98312 | tf_op jit(solution)/shard_map/ppermute | solution.py:383
  32.5 5.2 %collective-permute-start.8 = (f32[64,128]{1,0:T(8,128)S(1)}, f32[64,128]{1,0:T(8,128)S(1)}, u32[]{:S(2)}, u32[]{:S(2)}) collective-permute-start(f32[64,128]{1,0:T(8,128)S(1)} %get-tuple-element.27.own_ref), channel_id=1, source_target_pairs={{0,16},{4,20},{8,24},{12,28},{16,32},{20,36},{24,40},{28,44},{32,4... | collective-permute-start | bytes 98312 | tf_op jit(solution)/shard_map/ppermute | solution.py:383
  37.7 9.7 %collective-permute-start.9 = (f32[64,128]{1,0:T(8,128)S(1)}, f32[64,128]{1,0:T(8,128)S(1)}, u32[]{:S(2)}, u32[]{:S(2)}) collective-permute-start(f32[64,128]{1,0:T(8,128)S(1)} %get-tuple-element.29.own_ref), channel_id=1, source_target_pairs={{0,32},{4,36},{8,40},{12,44},{16,48},{20,52},{24,56},{28,60},{32,0... | collective-permute-start | bytes 98312 | tf_op jit(solution)/shard_map/ppermute | solution.py:383
  44.5 14.4 %collective-permute-start.15 = (f32[2,64,128]{2,1,0:T(8,128)S(1)}, f32[2,64,128]{2,1,0:T(8,128)S(1)}, u32[]{:S(2)}, u32[]{:S(2)}) collective-permute-start(f32[2,64,128]{2,1,0:T(8,128)S(1)} %get-tuple-element.34), channel_id=1, source_target_pairs={{0,1},{1,2},{2,3},{3,0},{4,5},{5,6},{6,7},{7,4},{8,9},{9,10},{10,1... | collective-permute-start | bytes 196616 | tf_op jit(solution)/shard_map/ppermute | solution.py:383
  44.7 14.1 %collective-permute-start.16 = (f32[2,64,128]{2,1,0:T(8,128)S(1)}, f32[2,64,128]{2,1,0:T(8,128)S(1)}, u32[]{:S(2)}, u32[]{:S(2)}) collective-permute-start(f32[2,64,128]{2,1,0:T(8,128)S(1)} %get-tuple-element.35), channel_id=1, source_target_pairs={{0,3},{1,0},{2,1},{3,2},{4,7},{5,4},{6,5},{7,6},{8,11},{9,8},{10,9... | collective-permute-start | bytes 196616 | tf_op jit(solution)/shard_map/ppermute | solution.py:383
  47.4 8.6 %collective-permute-start.10 = (f32[64,128]{1,0:T(8,128)S(1)}, f32[64,128]{1,0:T(8,128)S(1)}, u32[]{:S(2)}, u32[]{:S(2)}) collective-permute-start(f32[64,128]{1,0:T(8,128)S(1)} %shard_map.37.half_ref), channel_id=1, source_target_pairs={{0,4},{4,0},{8,12},{12,8},{16,20},{20,16},{24,28},{28,24},{32,36},... | collective-permute-start | bytes 98312 | tf_op jit(solution)/shard_map/ppermute | solution.py:387
where the time goes:
time: 63 us; the launch traced here: 62.9 us
  starting transfers between devices  32 us (51%)
  Pallas kernels  16.4 us (26%)
  waiting for transfers between devices  11.6 us (18%)
  local copies, waits for them, and re-layouts  2.19 us (3%)
  between operations  0.73 us (1%)
    ppermute x15, starting transfers between devices, shift(): return lax.ppermute(v, axis, [(i, (i + by) % n) for i in range(n)])  22.9 us
    ppermute x15, waiting for transfers between devices, shift(): return lax.ppermute(v, axis, [(i, (i + by) % n) for i in range(n)])  11.6 us
    ppermute x2, starting transfers between devices, partner(): lax.ppermute(v, 'gy', [(i, i ^ 1) for i in range(lax.axis_size('gy'))])  9.12 us
    pallas_call x1, Pallas kernels, box_z(): call(functools.partial(box_z_body, nb, sizes, scale), [w.shape], grid=(nx...  4.07 us
    pallas_call x1, Pallas kernels, local(): call(functools.partial(local_body, nb), [v.shape], grid=(nx // nb,), ins=...  3.39 us
    pallas_call x1, Pallas kernels, box_xy(): call(functools.partial(box_xy_body, nb, sizes), [v.shape, packed, packed]...  3 us
    pallas_call x1, Pallas kernels, last(): call(functools.partial(last_body, nb, scale), [s.shape], grid=(nx // nb,)...  2.79 us
    pallas_call x1, Pallas kernels, totals(): pl.pallas_call(functools.partial(totals_body, pieces), out_shape=[jax.Sha...  2.61 us
  transfers between devices with their start and end apart: 17, of which 4 were waited for; matrix products, arithmetic and copies ran while one was open for 0% of the time, Pallas kernels for 16%

commit v1 on v0

v1 whole, which is shorter than its diff:
```python
import functools
import math

import jax
import jax.numpy as jnp
from jax import lax
from jax.experimental import pallas as pl
from jax.experimental.pallas import tpu as pltpu
from jax.sharding import PartitionSpec as P


F32, BF16 = jnp.float32, jnp.bfloat16
MIB = 1 << 20


def iota(shape, dim):
    return lax.broadcasted_iota(jnp.int32, shape, dim)


def split(v):
    high = v.astype(BF16)
    return high, (v - high.astype(F32)).astype(BF16)


def ones_where(keep):
    return jnp.where(keep, 1.0, 0.0).astype(BF16)


def times(v, ones):
    parts, twice = jnp.concatenate(split(v), axis=1), jnp.concatenate([ones, ones], axis=0)
    return jnp.dot(parts, twice, preferred_element_type=F32)


def times_left(ones, v):
    high, low = split(v)
    dot = functools.partial(jnp.dot, preferred_element_type=F32)
    return dot(ones, high) + dot(ones, low)


def upper(n):
    return ones_where(iota((n, n), 0) <= iota((n, n), 1))


def lower(n):
    return ones_where(iota((n, n), 1) <= iota((n, n), 0))


def scan_rows(v):
    dim, n = v.ndim - 2, v.shape[-2]
    step = 1
    while step < n:
        if step < 8:
            moved = jnp.where(iota(v.shape, dim) >= step, pltpu.roll(v, step, dim), 0.0)
        else:
            kept = lax.slice_in_dim(v, 0, n - step, axis=dim)
            moved = jnp.concatenate([jnp.zeros_like(lax.slice_in_dim(v, 0, step, axis=dim)), kept], axis=dim)
        v = v + moved
        step *= 2
    return v


def five_rows(v):
    n = v.shape[0]
    two = v[: n - 1] + v[1:]
    four = two[: n - 3] + two[2:]
    return four[: n - 4] + v[4:]


def cost(flops, moved):
    return pl.CostEstimate(flops=flops, bytes_accessed=moved, transcendentals=0)


def call(body, out, grid=None, ins=None, outs=None, scratch=(), flops=1 << 20, moved=1 << 20, vmem=24):
    shapes = [jax.ShapeDtypeStruct(s, F32) for s in out]
    kw = {}
    if grid is not None:
        kw = dict(grid=grid, in_specs=ins, out_specs=outs)
    return pl.pallas_call(
        body,
        out_shape=shapes,
        scratch_shapes=list(scratch),
        compiler_params=pltpu.CompilerParams(vmem_limit_bytes=vmem * MIB),
        cost_estimate=cost(flops, moved),
        **kw,
    )


def whole(shape):
    return pl.BlockSpec(shape, lambda *_: (0,) * len(shape))


def xy_totals_body(pieces, v_ref, held_ref, rx_ref, ry_ref, near_ref, far_ref, sems):
    nx, ny, nz = held_ref.shape
    n = nx // pieces
    copies = [
        pltpu.make_async_copy(v_ref.at[pl.ds(k * n, n)], held_ref.at[pl.ds(k * n, n)], sems.at[k]) for k in range(pieces)
    ]
    for copy in copies:
        copy.start()

    def group(i, rx):
        rows = []
        for j in range(8):
            v = held_ref[i * 8 + j]
            rx = rx + v
            rows.append(jnp.sum(v, axis=0, keepdims=True))
        ry_ref[pl.ds(pl.multiple_of(i * 8, 8), 8), :] = jnp.concatenate(rows, axis=0)
        return rx

    rx = jnp.zeros((ny, nz), F32)
    for k, copy in enumerate(copies):
        copy.wait()
        rx = lax.fori_loop(k * n // 8, (k + 1) * n // 8, group, rx)
    rx_ref[...] = rx
    near_ref[...], far_ref[...] = facing("gx", held_ref[:2], held_ref[nx - 2 :])


def xy_totals(v):
    nx, ny, nz = v.shape
    pieces = 8
    return pl.pallas_call(
        functools.partial(xy_totals_body, pieces),
        out_shape=[jax.ShapeDtypeStruct(s, F32) for s in (v.shape, (ny, nz), (nx, nz), (2, ny, nz), (2, ny, nz))],
        in_specs=[pl.BlockSpec(memory_space=pltpu.HBM)],
        out_specs=[pl.BlockSpec(memory_space=pltpu.VMEM)] * 5,
        scratch_shapes=[pltpu.SemaphoreType.DMA((pieces,))],
        compiler_params=pltpu.CompilerParams(vmem_limit_bytes=48 * MIB),
        cost_estimate=cost(6 << 20, 8 << 20),
    )(v)


def z_totals_body(v_ref, rz_ref):
    nx, ny, _ = v_ref.shape
    lane = iota((ny, nx), 1)

    def group(i, rz):
        for j in range(8):
            rz = jnp.where(lane == i * 8 + j, jnp.sum(v_ref[i * 8 + j], axis=1, keepdims=True), rz)
        return rz

    rz_ref[...] = lax.fori_loop(0, nx // 8, group, jnp.zeros((ny, nx), F32))


def merge_body(axis, bit, from_ref, own_ref, *refs):
    got = from_ref[...]
    *low_ref, low_out, own_out = refs
    low = jnp.where(lax.rem(lax.shift_right_logical(lax.axis_index(axis), bit), 2) == 1, got, 0.0)
    low_out[...] = low + low_ref[0][...] if low_ref else low
    own_out[...] = own_ref[...] + got


def merge(axis, bit, got, own, *low):
    return call(functools.partial(merge_body, axis, bit), [own.shape] * 2)(got, own, *low)


def high_bit(axis, bit, got_ref, low_ref):
    return low_ref[...] + jnp.where(lax.shift_right_logical(lax.axis_index(axis), bit) == 1, got_ref[...], 0.0)


def spread_body(ry_ref, out_ref):
    ry = ry_ref[...]
    out_ref[...] = times_left(lower(ry.shape[0]), times(ry, upper(ry.shape[1])))


def after_x_body(got_ref, low_ref, rz_ref, cx_ref, out_ref):
    cx = high_bit("gx", 1, got_ref, low_ref)
    cx_ref[...] = cx
    rz = rz_ref[...]
    out_ref[...] = rz + jnp.where(iota(rz.shape, 1) == 0, jnp.sum(cx, axis=1, keepdims=True), 0.0)


def after_z_body(got_ref, low_ref, cx_ref, ry_ref, cz_ref, out_ref):
    cz = high_bit("gz", 1, got_ref, low_ref)
    cz_ref[...] = cz
    nx, nz = ry_ref.shape
    row = jnp.sum(cz, axis=0, keepdims=True)
    column = jnp.sum(jnp.where(iota((nx, nx), 1) <= iota((nx, nx), 0), row, 0.0), axis=1, keepdims=True)
    along = times(jnp.broadcast_to(jnp.sum(cx_ref[...], axis=0, keepdims=True), (8, nz)), upper(nz))
    out_ref[...] = ry_ref[...] + column + along[:1]


def pair_body(mine_ref, other_ref, out_ref):
    core = lax.rem(lax.axis_index("gy"), 2)
    n = out_ref.shape[0]
    both = mine_ref[...] + other_ref[...]
    out_ref[...] = jnp.where(core == 0, both[:n], both[n:])


def after_y_body(got_ref, low_ref, out_ref):
    out_ref[...] = high_bit("gy", 3, got_ref, low_ref)


def local_body(nb, v_ref, cz_ref, cx_ref, out_ref, acc):
    i = pl.program_id(0)
    ny, nz = acc.shape
    up = upper(nz)

    @pl.when(i == 0)
    def _():
        acc[...] = scan_rows(times(cx_ref[...], up))

    lane = iota((ny, nz), 1)
    cz = cz_ref[...]
    rows = []
    for j in range(nb):
        x = i * nb + j
        rows.append(v_ref[j] + jnp.where(lane == 0, pltpu.roll(cz, lax.rem(nz - x, nz), 1), 0.0))
    along = times(jnp.concatenate(rows, axis=0), up).reshape(nb, ny, nz)
    total = acc[...]
    for j in range(nb):
        total = total + scan_rows(along[j])
        out_ref[j] = total
    acc[...] = total


def local(v, cz, cx):
    nx, ny, nz = v.shape
    nb = 32
    return call(
        functools.partial(local_body, nb),
        [v.shape],
        grid=(nx // nb,),
        ins=[pl.BlockSpec((nb, ny, nz), lambda i: (i, 0, 0)), whole(cz.shape), whole(cx.shape)],
        outs=[pl.BlockSpec((nb, ny, nz), lambda i: (i, 0, 0))],
        scratch=[pltpu.VMEM((ny, nz), F32)],
        flops=1 << 29,
        moved=8 << 20,
    )(v, cz, cx)[0]


def last_body(pieces, scale, s_ref, half_ref, other_half_ref, partner_ref, out_ref, gy, made, sems):
    core = lax.rem(lax.axis_index("gy"), 2)
    n = half_ref.shape[0]
    mine, other = half_ref[...], other_half_ref[...]
    for k in range(2):
        part = jnp.where(core == k, mine, other)
        gy[k * n : (k + 1) * n] = part + jnp.where(core == 1, partner_ref[k * n : (k + 1) * n], 0.0)
    n = made.shape[0] // pieces
    copies = []
    for k in range(pieces):

        def group(i, _):
            rows = gy[pl.ds(pl.multiple_of(i * 8, 8), 8), :]
            for j in range(8):
                made[i * 8 + j] = (s_ref[i * 8 + j] + rows[j : j + 1]) * scale
            return 0

        lax.fori_loop(k * n // 8, (k + 1) * n // 8, group, 0)
        copies.append(pltpu.make_async_copy(made.at[pl.ds(k * n, n)], out_ref.at[pl.ds(k * n, n)], sems.at[k]))
        copies[k].start()
    for copy in copies:
        copy.wait()


def last(s, half, other_half, partner, scale):
    nx, _, nz = s.shape
    pieces = 8
    return pl.pallas_call(
        functools.partial(last_body, pieces, scale),
        out_shape=jax.ShapeDtypeStruct(s.shape, F32),
        in_specs=[pl.BlockSpec(memory_space=pltpu.VMEM)] * 4,
        out_specs=pl.BlockSpec(memory_space=pltpu.HBM),
        scratch_shapes=[pltpu.VMEM((nx, nz), F32), pltpu.VMEM(s.shape, F32), pltpu.SemaphoreType.DMA((pieces,))],
        compiler_params=pltpu.CompilerParams(vmem_limit_bytes=24 * MIB),
        cost_estimate=cost(1 << 24, 8 << 20),
    )(s, half, other_half, partner)


def sides(axis, near, far):
    own = lax.axis_index(axis)
    even = lax.rem(own, 2) == 0
    lower = jnp.where(own > 0, jnp.where(even, far, near), 0.0)
    return lower, jnp.where(own < lax.axis_size(axis) - 1, jnp.where(even, near, far), 0.0)


def facing(axis, first, final):
    even = lax.rem(lax.axis_index(axis), 2) == 0
    return jnp.where(even, final, first), jnp.where(even, first, final)


def strips_body(first_ref, last_ref, near_a, far_a, near_b, far_b, near_ref, far_ref):
    for layer in range(2):
        made = []
        for v_ref, near, far, y in ((first_ref, near_a, far_a, layer), (last_ref, near_b, far_b, 6 + layer)):
            lo, hi = sides("gx", near[:, y, :], far[:, y, :])
            made.append(five_rows(jnp.concatenate([lo, v_ref[:, y, :], hi], axis=0)))
        near_ref[layer], far_ref[layer] = facing("gy", *made)


def strips(v, x_near, x_far):
    nx, ny, nz = v.shape
    end = ny // 8 - 1
    at_first, at_last = lambda i: (0, 0, 0), lambda i: (0, end, 0)
    return call(
        strips_body,
        [(2, nx, nz), (2, nx, nz)],
        grid=(1,),
        ins=[
            pl.BlockSpec((nx, 8, nz), at_first),
            pl.BlockSpec((nx, 8, nz), at_last),
            pl.BlockSpec((2, 8, nz), at_first),
            pl.BlockSpec((2, 8, nz), at_first),
            pl.BlockSpec((2, 8, nz), at_last),
            pl.BlockSpec((2, 8, nz), at_last),
        ],
        outs=[whole((2, nx, nz)), whole((2, nx, nz))],
        flops=1 << 22,
        moved=2 << 20,
    )(v, v, x_near, x_far, x_near, x_far)


def box_xy_body(nb, v_ref, x_near, x_far, y_near, y_far, out_ref, near_ref, far_ref):
    i = pl.program_id(0)
    steps = pl.num_programs(0)
    ny, nz = v_ref.shape[1:]
    base = pl.multiple_of(i * nb, nb)
    group = lax.div(i * nb * 2, nz)

    def run(first, final):
        def row(j):
            if first and j < 0:
                return sides("gx", x_near[j + 2], x_far[j + 2])[0]
            if final and j >= nb:
                return sides("gx", x_near[j - nb], x_far[j - nb])[1]
            return v_ref[base + j]

        lane = iota((ny, nz), 1)
        pairs = [sides("gy", y_near[k, pl.ds(base, nb), :], y_far[k, pl.ds(base, nb), :]) for k in range(2)]
        lows, highs = zip(*pairs)
        up = jnp.zeros((ny, nz), F32)
        down = jnp.zeros((ny, nz), F32)
        twos = {j: row(j) + row(j + 1) for j in range(-2, nb + 1)}
        for j in range(nb):
            along = twos[j - 2] + twos[j] + row(j + 2)
            ext = jnp.concatenate(
                [lows[0][j : j + 1], lows[1][j : j + 1], along, highs[0][j : j + 1], highs[1][j : j + 1]], axis=0
            )
            box = five_rows(ext)
            out_ref[j] = box
            at = lax.rem(base + j, nz // 2) * 2
            here = lax.div(lane, 2) * 2 == at
            up = jnp.where(here, pltpu.roll(box, lax.rem(at + 2, nz), 1), up)
            down = jnp.where(here, pltpu.roll(box, at, 1), down)
        at0 = lax.rem(base, nz // 2) * 2
        mine = jnp.logical_and(lane >= at0, lane < at0 + 2 * nb)
        near, far = facing("gz", down, up)
        near_ref[group] = jnp.where(mine, near, near_ref[group])
        far_ref[group] = jnp.where(mine, far, far_ref[group])

    pl.when(i == 0)(lambda: run(True, False))
    pl.when(i == steps - 1)(lambda: run(False, True))
    pl.when(jnp.logical_and(i > 0, i < steps - 1))(lambda: run(False, False))


def box_xy(v, x_near, x_far, y_near, y_far):
    nx, ny, nz = v.shape
    nb = 32
    packed = (2 * nx // nz, ny, nz)
    return call(
        functools.partial(box_xy_body, nb),
        [v.shape, packed, packed],
        grid=(nx // nb,),
        ins=[whole(v.shape), whole(x_near.shape), whole(x_far.shape), whole(y_near.shape), whole(y_far.shape)],
        outs=[pl.BlockSpec((nb, ny, nz), lambda i: (i, 0, 0)), whole(packed), whole(packed)],
        flops=1 << 26,
        moved=8 << 20,
    )(v, x_near, x_far, y_near, y_far)


def box_z_body(nb, scale, w_ref, near_ref, far_ref, out_ref, both):
    i = pl.program_id(0)
    ny, nz = w_ref.shape[1:]
    lane = iota((ny, nz), 1)

    @pl.when(i == 0)
    def _():
        source, target = iota((nz, nz), 0), iota((nz, nz), 1)
        even = lax.rem(lane, 2) == 0
        for g in range(near_ref.shape[0]):
            lo, hi = sides("gz", near_ref[g], far_ref[g])
            lo = lo + jnp.where(even, pltpu.roll(lo, nz - 1, 1), 0.0)
            hi = hi + jnp.where(even, 0.0, pltpu.roll(hi, 1, 1))
            for k in range(2):
                place = lax.div(source, 2) * 4 + lax.rem(source, 2) - k * nz
                both[2 * g + k] = times(hi, ones_where(target == place)) + times(lo, ones_where(target == place + 2))

    away = iota((nz, nz), 0) - iota((nz, nz), 1)
    band = ones_where(jnp.logical_and(away <= 2, away >= -2))
    along = times(w_ref[...].reshape(nb * ny, nz), band).reshape(nb, ny, nz)
    edge = jnp.logical_or(lane < 2, lane >= nz - 2)
    side = both[i]
    for j in range(nb):
        out_ref[j] = (along[j] + jnp.where(edge, pltpu.roll(side, (2 * nz - 2 - 4 * j) % nz, 1), 0.0)) * scale


def box_z(w, near, far, scale):
    nx, ny, nz = w.shape
    nb = nz // 4
    return call(
        functools.partial(box_z_body, nb, scale),
        [w.shape],
        grid=(nx // nb,),
        ins=[pl.BlockSpec((nb, ny, nz), lambda i: (i, 0, 0)), whole(near.shape), whole(far.shape)],
        outs=[pl.BlockSpec((nb, ny, nz), lambda i: (i, 0, 0))],
        scratch=[pltpu.VMEM((nx // nb, ny, nz), F32)],
        flops=1 << 29,
        moved=8 << 20,
    )(w, near, far)[0]


def swap(v, axis, mask):
    return lax.ppermute(v, axis, [(i, i ^ mask) for i in range(lax.axis_size(axis))])


def away(v, axis):
    n = lax.axis_size(axis)
    return lax.ppermute(v, axis, [(i, (i + 2 * (i % 2) - 1) % n) for i in range(n)])


def per_device(v):
    nx, ny, nz = v.shape
    cells = nx * ny * nz * lax.axis_size("gx") * lax.axis_size("gy") * lax.axis_size("gz")

    held, rx, ry, near, far = xy_totals(v)

    got = swap(rx, "gx", 1)
    x_near, x_far = swap(near, "gx", 1), away(far, "gx")
    low, own = merge("gx", 0, got, rx)
    got = swap(own, "gx", 3)
    (rz,) = call(z_totals_body, [(ny, nx)])(held)
    (ry,) = call(spread_body, [ry.shape])(ry)
    cx, rz = call(after_x_body, [rx.shape, rz.shape])(got, low, rz)

    got = swap(rz, "gz", 1)
    near, far = strips(held, x_near, x_far)
    y_near, y_far = swap(near, "gy", 1), away(far, "gy")
    low, own = merge("gz", 0, got, rz)
    got = swap(own, "gz", 3)
    w, near, far = box_xy(held, x_near, x_far, y_near, y_far)
    cz, ry = call(after_z_body, [rz.shape, ry.shape])(got, low, cx, ry)

    other = swap(ry, "gy", 1)
    (own,) = call(pair_body, [(nx // 2, nz)])(ry, other)
    got = swap(own, "gy", 2)
    z_near, z_far = swap(near, "gz", 1), away(far, "gz")
    low, own = merge("gy", 1, got, own)
    got = swap(own, "gy", 6)
    s = local(held, cz, cx)
    low, own = merge("gy", 2, got, own, low)
    got = swap(own, "gy", 14)
    box_sum = box_z(w, z_near, z_far, 1.0 / math.sqrt(125.0))
    (low,) = call(after_y_body, [low.shape])(got, low)
    other_low = swap(low, "gy", 1)
    prefix = last(s, low, other_low, other, 1.0 / math.sqrt(cells))
    return (prefix, box_sum)


def solution(mesh):
    return jax.shard_map(
        per_device,
        mesh=mesh,
        in_specs=(P("gx", "gy", "gz"),),
        out_specs=(P("gx", "gy", "gz"), P("gx", "gy", "gz")),
        check_vma=False,
    )
```

time: 63 us -> 52.7 us (0.84)
  waiting for transfers between devices: 11.6 us -> 6.75 us
  starting transfers between devices: 32 us -> 27.4 us
  local copies, waits for them, and re-layouts: 2.19 us -> 0 us
  Pallas kernels: 16.4 us -> 17.7 us
    ppermute x17 -> x15, waiting for transfers between devices: 11.6 us -> 6.75 us  [the longest x12 6.74 us: swap(): lax.ppermute(v, axis, [(i, i ^ mask) for i in range(lax.axis_size(axis))])]
    ppermute x17 -> x15, starting transfers between devices: 32 us -> 27.4 us  [the longest x12 24.7 us: swap(): lax.ppermute(v, axis, [(i, i ^ mask) for i in range(lax.axis_size(axis))])]
    unnamed x2 -> x0, local copies, waits for them, and re-layouts: 2.18 us -> none
    pallas_call x11 -> x15, Pallas kernels: 13 us -> 14.3 us  [the longest x1 3.63 us: box_z(): call(functools.partial(box_z_body, nb, scale), [w.shape], grid=(nx // nb,...]
  transfers between devices with their start and end apart: 17 -> 15, of which waited for: 4 -> 4; matrix products, arithmetic and copies ran while one was open for 0% -> 0% of each run, Pallas kernels for 16% -> 25%
where the time goes in v1:
time: 52.7 us; the launch traced here: 52.6 us
  starting transfers between devices  27.4 us (52%)
  Pallas kernels  17.7 us (34%)
  waiting for transfers between devices  6.75 us (13%)
  between operations  0.76 us (1%)
    ppermute x12, starting transfers between devices, swap(): lax.ppermute(v, axis, [(i, i ^ mask) for i in range(lax.axis_size(axis))])  24.7 us
    ppermute x12, waiting for transfers between devices, swap(): lax.ppermute(v, axis, [(i, i ^ mask) for i in range(lax.axis_size(axis))])  6.74 us
    pallas_call x1, Pallas kernels, box_z(): call(functools.partial(box_z_body, nb, scale), [w.shape], grid=(nx // nb,...  3.63 us
    pallas_call x1, Pallas kernels, local(): call(functools.partial(local_body, nb), [v.shape], grid=(nx // nb,), ins=...  3.38 us
    pallas_call x1, Pallas kernels, box_xy(): call(functools.partial(box_xy_body, nb), [v.shape, packed, packed], grid=...  3.03 us
    ppermute x3, starting transfers between devices, away(): lax.ppermute(v, axis, [(i, (i + 2 * (i % 2) - 1) % n) for i in range(n)])  2.69 us
    pallas_call x1, Pallas kernels, xy_totals(): pl.pallas_call(functools.partial(xy_totals_body, pieces), out_shape=[jax....  2.3 us
    pallas_call x1, Pallas kernels, per_device(): rz, = call(z_totals_body, [(ny, nx)])(held)  2.26 us
  transfers between devices with their start and end apart: 15, of which 4 were waited for; matrix products, arithmetic and copies ran while one was open for 0% of the time, Pallas kernels for 25%

profile of v1, /device:TPU:1, one launch (start us, length us, event | category | flops | bytes accessed | tf_op | source)
XLA Modules:
  0.0 52.6 jit_solution(17081935353383978000)
XLA Ops:
  0.6 2.3 %shard_map.30 = (f32[128,64,128]{2,1,0:T(8,128)S(1)}, f32[64,128]{1,0:T(8,128)S(1)}, f32[128,128]{1,0:T(8,128)S(1)}, f32[2,64,128]{2,1,0:T(8,128)S(1)}, f32[2,64,128]{2,1,0:T(8,128)S(1)}) custom-call(f32[128,64,128]{2,1,0:T(8,128)} %v_ref.1), custom_call_target="tpu_custom_call" | custom-call | flops 6291456 | bytes 8388608 | tf_op jit(solution)/shard_map/pallas_call | solution.py:121
  2.9 2.1 %collective-permute-start = (f32[64,128]{1,0:T(8,128)S(1)}, f32[64,128]{1,0:T(8,128)S(1)}, u32[]{:S(2)}, u32[]{:S(2)}) collective-permute-start(f32[64,128]{1,0:T(8,128)S(1)} %get-tuple-element.25.own_ref), channel_id=1, source_target_pairs={{0,64},{64,0},{128,192},{192,128},{1,65},{65,1},{129,193},{193,129... | collective-permute-start | bytes 98312 | tf_op jit(solution)/shard_map/ppermute | solution.py:412
  5.0 1.3 %collective-permute-done.from_ref = f32[64,128]{1,0:T(8,128)S(1)} collective-permute-done((f32[64,128]{1,0:T(8,128)S(1)}, f32[64,128]{1,0:T(8,128)S(1)}, u32[]{:S(2)}, u32[]{:S(2)}) %collective-permute-start) | collective-permute-done | bytes 32800 | tf_op jit(solution)/shard_map/ppermute | solution.py:412
  6.4 2.8 %collective-permute-start.1 = (f32[64,128]{1,0:T(8,128)S(1)}, f32[64,128]{1,0:T(8,128)S(1)}, u32[]{:S(2)}, u32[]{:S(2)}) collective-permute-start(f32[64,128]{1,0:T(8,128)S(1)} %get-tuple-element.26), channel_id=1, source_target_pairs={{0,192},{64,128},{128,64},{192,0},{1,193},{65,129},{129,65},{193,1... | collective-permute-start | bytes 98312 | tf_op jit(solution)/shard_map/ppermute | solution.py:412
  9.2 0.1 collective-permute-start.10
  9.3 0.1 collective-permute-start.9
  9.4 2.3 %shard_map.32.rz_ref = f32[64,128]{1,0:T(8,128)S(1)} custom-call(f32[128,64,128]{2,1,0:T(8,128)S(1)} %get-tuple-element.24.v_ref.first_ref.last_ref), custom_call_target="tpu_custom_call" | custom-call | flops 1048576 | bytes 1048576 | tf_op jit(solution)/shard_map/pallas_call | solution.py:430
  11.6 0.0 collective-permute-done.1.got_ref
  11.7 0.1 shard_map.33
  11.8 1.3 %collective-permute-start.2 = (f32[64,128]{1,0:T(8,128)S(1)}, f32[64,128]{1,0:T(8,128)S(1)}, u32[]{:S(2)}, u32[]{:S(2)}) collective-permute-start(f32[64,128]{1,0:T(8,128)S(1)} %get-tuple-element.28.own_ref), channel_id=1, source_target_pairs={{0,1},{1,0},{2,3},{3,2},{4,5},{5,4},{6,7},{7,6},{8,9},{9,8},{10,11... | collective-permute-start | bytes 98312 | tf_op jit(solution)/shard_map/ppermute | solution.py:412
  13.1 1.8 %collective-permute-done.2.from_ref = f32[64,128]{1,0:T(8,128)S(1)} collective-permute-done((f32[64,128]{1,0:T(8,128)S(1)}, f32[64,128]{1,0:T(8,128)S(1)}, u32[]{:S(2)}, u32[]{:S(2)}) %collective-permute-start.2) | collective-permute-done | bytes 32800 | tf_op jit(solution)/shard_map/ppermute | solution.py:412
  14.9 2.5 %collective-permute-start.3 = (f32[64,128]{1,0:T(8,128)S(1)}, f32[64,128]{1,0:T(8,128)S(1)}, u32[]{:S(2)}, u32[]{:S(2)}) collective-permute-start(f32[64,128]{1,0:T(8,128)S(1)} %get-tuple-element.29), channel_id=1, source_target_pairs={{0,3},{1,2},{2,1},{3,0},{4,7},{5,6},{6,5},{7,4},{8,11},{9,10},{10,... | collective-permute-start | bytes 98312 | tf_op jit(solution)/shard_map/ppermute | solution.py:412
  17.4 0.0 collective-permute-done.10.far_a.far_b.x_far
  17.4 0.0 collective-permute-done.9.near_a.near_b.x_near
  17.4 0.3 shard_map.43
  17.7 4.2 %collective-permute-start.11 = (f32[2,128,128]{2,1,0:T(8,128)S(1)}, f32[2,128,128]{2,1,0:T(8,128)S(1)}, u32[]{:S(2)}, u32[]{:S(2)}) collective-permute-start(f32[2,128,128]{2,1,0:T(8,128)S(1)} %get-tuple-element.41), channel_id=1, source_target_pairs={{0,4},{4,0},{8,12},{12,8},{16,20},{20,16},{24,28},{28,24},{32,36},... | collective-permute-start | bytes 393224 | tf_op jit(solution)/shard_map/ppermute | solution.py:412
  21.9 1.6 %collective-permute-start.12 = (f32[2,128,128]{2,1,0:T(8,128)S(1)}, f32[2,128,128]{2,1,0:T(8,128)S(1)}, u32[]{:S(2)}, u32[]{:S(2)}) collective-permute-start(f32[2,128,128]{2,1,0:T(8,128)S(1)} %get-tuple-element.42), channel_id=1, source_target_pairs={{0,60},{4,8},{8,4},{12,16},{16,12},{20,24},{24,20},{28,32},{32,28}... | collective-permute-start | bytes 393224 | tf_op jit(solution)/shard_map/ppermute | solution.py:417
  23.5 0.3 shard_map.35.ry_ref
  23.9 0.0 collective-permute-done.3.got_ref
  23.9 0.1 shard_map.36
  24.0 4.4 %collective-permute-start.4 = (f32[128,128]{1,0:T(8,128)S(1)}, f32[128,128]{1,0:T(8,128)S(1)}, u32[]{:S(2)}, u32[]{:S(2)}) collective-permute-start(f32[128,128]{1,0:T(8,128)S(1)} %get-tuple-element.34.mine_ref), channel_id=1, source_target_pairs={{0,4},{4,0},{8,12},{12,8},{16,20},{20,16},{24,28},{28,24},{32,36},... | collective-permute-start | bytes 196616 | tf_op jit(solution)/shard_map/ppermute | solution.py:412
  28.4 0.9 %collective-permute-done.4.other_ref.partner_ref = f32[128,128]{1,0:T(8,128)S(1)} collective-permute-done((f32[128,128]{1,0:T(8,128)S(1)}, f32[128,128]{1,0:T(8,128)S(1)}, u32[]{:S(2)}, u32[]{:S(2)}) %collective-permute-start.4) | collective-permute-done | bytes 65568 | tf_op jit(solution)/shard_map/ppermute | solution.py:412
  29.4 0.1 collective-permute-start.5
  29.5 2.8 %collective-permute-done.5.from_ref = f32[64,128]{1,0:T(8,128)S(1)} collective-permute-done((f32[64,128]{1,0:T(8,128)S(1)}, f32[64,128]{1,0:T(8,128)S(1)}, u32[]{:S(2)}, u32[]{:S(2)}) %collective-permute-start.5) | collective-permute-done | bytes 32800 | tf_op jit(solution)/shard_map/ppermute | solution.py:412
  32.2 1.6 %collective-permute-start.6 = (f32[64,128]{1,0:T(8,128)S(1)}, f32[64,128]{1,0:T(8,128)S(1)}, u32[]{:S(2)}, u32[]{:S(2)}) collective-permute-start(f32[64,128]{1,0:T(8,128)S(1)} %get-tuple-element.35.own_ref), channel_id=1, source_target_pairs={{0,24},{4,28},{8,16},{12,20},{16,8},{20,12},{24,0},{28,4},{32,56},... | collective-permute-start | bytes 98312 | tf_op jit(solution)/shard_map/ppermute | solution.py:412
  33.9 0.0 collective-permute-done.11.y_near
  33.9 0.0 collective-permute-done.12.y_far
  33.9 3.0 %shard_map.44 = (f32[128,64,128]{2,1,0:T(8,128)S(1)}, f32[2,64,128]{2,1,0:T(8,128)S(1)}, f32[2,64,128]{2,1,0:T(8,128)S(1)}) custom-call(f32[128,64,128]{2,1,0:T(8,128)S(1)} %get-tuple-element.24.v_ref.first_ref.last_ref, f32[2,64,128]{2,1,0:T(8,128)S(1)} %collective-permute-done.9.near_a.near_b.x_near, ...), custom_call_target="tpu_custom_call" | custom-call | flops 67108864 | bytes 8388608 | tf_op jit(solution)/shard_map/pallas_call | solution.py:359
  36.9 0.1 collective-permute-start.13
  37.0 1.0 %collective-permute-start.14 = (f32[2,64,128]{2,1,0:T(8,128)S(1)}, f32[2,64,128]{2,1,0:T(8,128)S(1)}, u32[]{:S(2)}, u32[]{:S(2)}) collective-permute-start(f32[2,64,128]{2,1,0:T(8,128)S(1)} %get-tuple-element.45), channel_id=1, source_target_pairs={{0,3},{1,2},{2,1},{3,0},{4,7},{5,6},{6,5},{7,4},{8,11},{9,10},{10,... | collective-permute-start | bytes 196616 | tf_op jit(solution)/shard_map/ppermute | solution.py:417
  38.0 0.0 collective-permute-done.6.from_ref
  38.0 2.9 %collective-permute-start.7 = (f32[64,128]{1,0:T(8,128)S(1)}, f32[64,128]{1,0:T(8,128)S(1)}, u32[]{:S(2)}, u32[]{:S(2)}) collective-permute-start(f32[64,128]{1,0:T(8,128)S(1)} %get-tuple-element.37), channel_id=1, source_target_pairs={{0,56},{4,60},{8,48},{12,52},{16,40},{20,44},{24,32},{28,36},{32,2... | collective-permute-start | bytes 98312 | tf_op jit(solution)/shard_map/ppermute | solution.py:412
  40.9 3.4 %shard_map.37.s_ref = f32[128,64,128]{2,1,0:T(8,128)S(1)} custom-call(f32[128,64,128]{2,1,0:T(8,128)S(1)} %get-tuple-element.24.v_ref.first_ref.last_ref, f32[64,128]{1,0:T(8,128)S(1)} %get-tuple-element.33.cz_ref, f32[64,128]{1,0:T(8,128)S(1)} %get-tuple-element.31.cx_ref), custom_call_target="tpu_custom_call" | custom-call | flops 536870912 | bytes 8388608 | tf_op jit(solution)/shard_map/pallas_call | solution.py:219
  44.3 0.0 collective-permute-done.7.got_ref
  44.4 2.4 %collective-permute-start.8 = (f32[64,128]{1,0:T(8,128)S(1)}, f32[64,128]{1,0:T(8,128)S(1)}, u32[]{:S(2)}, u32[]{:S(2)}) collective-permute-start(f32[64,128]{1,0:T(8,128)S(1)} %shard_map.41.half_ref), channel_id=1, source_target_pairs={{0,4},{4,0},{8,12},{12,8},{16,20},{20,16},{24,28},{28,24},{32,36},... | collective-permute-start | bytes 98312 | tf_op jit(solution)/shard_map/ppermute | solution.py:412
  46.8 0.0 collective-permute-done.13.near_ref
  46.8 0.0 collective-permute-done.14.far_ref
  46.8 3.6 %shard_map.45 = f32[128,64,128]{2,1,0:T(8,128)} custom-call(f32[128,64,128]{2,1,0:T(8,128)S(1)} %get-tuple-element.43.w_ref, f32[2,64,128]{2,1,0:T(8,128)S(1)} %collective-permute-done.13.near_ref, f32[2,64,128]{2,1,0:T(8,128)S(1)} %collective-permute-done.14.far_ref), custom_call_target="tpu_custom_call" | custom-call | flops 536870912 | bytes 8388608 | tf_op jit(solution)/shard_map/pallas_call | solution.py:399
  50.4 0.0 collective-permute-done.8.other_half_ref
  50.4 2.1 %shard_map.42 = f32[128,64,128]{2,1,0:T(8,128)} custom-call(f32[128,64,128]{2,1,0:T(8,128)S(1)} %shard_map.37.s_ref, f32[64,128]{1,0:T(8,128)S(1)} %shard_map.41.half_ref, f32[64,128]{1,0:T(8,128)S(1)} %collective-permute-done.8.other_half_ref, f32[128,128]{1,0:T(8,128)S(1)} %collective-permute-done.4.other_ref.partner_ref), custom_call_target="tpu_custom_call" | custom-call | flops 16777216 | bytes 8388608 | tf_op jit(solution)/shard_map/pallas_call | solution.py:258
  (6 shorter events, 0.1 us)
Async XLA Ops:
  2.9 3.4 %collective-permute-start = (f32[64,128]{1,0:T(8,128)S(1)}, f32[64,128]{1,0:T(8,128)S(1)}, u32[]{:S(2)}, u32[]{:S(2)}) collective-permute-start(f32[64,128]{1,0:T(8,128)S(1)} %get-tuple-element.25.own_ref), channel_id=1, source_target_pairs={{0,64},{64,0},{128,192},{192,128},{1,65},{65,1},{129,193},{193,129... | collective-permute-start | bytes 98312 | tf_op jit(solution)/shard_map/ppermute | solution.py:412
  6.4 5.3 %collective-permute-start.1 = (f32[64,128]{1,0:T(8,128)S(1)}, f32[64,128]{1,0:T(8,128)S(1)}, u32[]{:S(2)}, u32[]{:S(2)}) collective-permute-start(f32[64,128]{1,0:T(8,128)S(1)} %get-tuple-element.26), channel_id=1, source_target_pairs={{0,192},{64,128},{128,64},{192,0},{1,193},{65,129},{129,65},{193,1... | collective-permute-start | bytes 98312 | tf_op jit(solution)/shard_map/ppermute | solution.py:412
  9.2 8.2 %collective-permute-start.10 = (f32[2,64,128]{2,1,0:T(8,128)S(1)}, f32[2,64,128]{2,1,0:T(8,128)S(1)}, u32[]{:S(2)}, u32[]{:S(2)}) collective-permute-start(f32[2,64,128]{2,1,0:T(8,128)S(1)} %get-tuple-element.40), channel_id=1, source_target_pairs={{0,192},{64,128},{128,64},{192,0},{1,193},{65,129},{129,65},{193,1... | collective-permute-start | bytes 196616 | tf_op jit(solution)/shard_map/ppermute | solution.py:417
  9.3 8.1 %collective-permute-start.9 = (f32[2,64,128]{2,1,0:T(8,128)S(1)}, f32[2,64,128]{2,1,0:T(8,128)S(1)}, u32[]{:S(2)}, u32[]{:S(2)}) collective-permute-start(f32[2,64,128]{2,1,0:T(8,128)S(1)} %get-tuple-element.39), channel_id=1, source_target_pairs={{0,64},{64,0},{128,192},{192,128},{1,65},{65,1},{129,193},{193,129... | collective-permute-start | bytes 196616 | tf_op jit(solution)/shard_map/ppermute | solution.py:412
  11.8 3.1 %collective-permute-start.2 = (f32[64,128]{1,0:T(8,128)S(1)}, f32[64,128]{1,0:T(8,128)S(1)}, u32[]{:S(2)}, u32[]{:S(2)}) collective-permute-start(f32[64,128]{1,0:T(8,128)S(1)} %get-tuple-element.28.own_ref), channel_id=1, source_target_pairs={{0,1},{1,0},{2,3},{3,2},{4,5},{5,4},{6,7},{7,6},{8,9},{9,8},{10,11... | collective-permute-start | bytes 98312 | tf_op jit(solution)/shard_map/ppermute | solution.py:412
  14.9 9.0 %collective-permute-start.3 = (f32[64,128]{1,0:T(8,128)S(1)}, f32[64,128]{1,0:T(8,128)S(1)}, u32[]{:S(2)}, u32[]{:S(2)}) collective-permute-start(f32[64,128]{1,0:T(8,128)S(1)} %get-tuple-element.29), channel_id=1, source_target_pairs={{0,3},{1,2},{2,1},{3,0},{4,7},{5,6},{6,5},{7,4},{8,11},{9,10},{10,... | collective-permute-start | bytes 98312 | tf_op jit(solution)/shard_map/ppermute | solution.py:412
  17.7 16.1 %collective-permute-start.11 = (f32[2,128,128]{2,1,0:T(8,128)S(1)}, f32[2,128,128]{2,1,0:T(8,128)S(1)}, u32[]{:S(2)}, u32[]{:S(2)}) collective-permute-start(f32[2,128,128]{2,1,0:T(8,128)S(1)} %get-tuple-element.41), channel_id=1, source_target_pairs={{0,4},{4,0},{8,12},{12,8},{16,20},{20,16},{24,28},{28,24},{32,36},... | collective-permute-start | bytes 393224 | tf_op jit(solution)/shard_map/ppermute | solution.py:412
  21.9 12.0 %collective-permute-start.12 = (f32[2,128,128]{2,1,0:T(8,128)S(1)}, f32[2,128,128]{2,1,0:T(8,128)S(1)}, u32[]{:S(2)}, u32[]{:S(2)}) collective-permute-start(f32[2,128,128]{2,1,0:T(8,128)S(1)} %get-tuple-element.42), channel_id=1, source_target_pairs={{0,60},{4,8},{8,4},{12,16},{16,12},{20,24},{24,20},{28,32},{32,28}... | collective-permute-start | bytes 393224 | tf_op jit(solution)/shard_map/ppermute | solution.py:417
  24.0 5.3 %collective-permute-start.4 = (f32[128,128]{1,0:T(8,128)S(1)}, f32[128,128]{1,0:T(8,128)S(1)}, u32[]{:S(2)}, u32[]{:S(2)}) collective-permute-start(f32[128,128]{1,0:T(8,128)S(1)} %get-tuple-element.34.mine_ref), channel_id=1, source_target_pairs={{0,4},{4,0},{8,12},{12,8},{16,20},{20,16},{24,28},{28,24},{32,36},... | collective-permute-start | bytes 196616 | tf_op jit(solution)/shard_map/ppermute | solution.py:412
  29.4 2.9 %collective-permute-start.5 = (f32[64,128]{1,0:T(8,128)S(1)}, f32[64,128]{1,0:T(8,128)S(1)}, u32[]{:S(2)}, u32[]{:S(2)}) collective-permute-start(f32[64,128]{1,0:T(8,128)S(1)} %shard_map.38.own_ref), channel_id=1, source_target_pairs={{0,8},{4,12},{8,0},{12,4},{16,24},{20,28},{24,16},{28,20},{32,40},... | collective-permute-start | bytes 98312 | tf_op jit(solution)/shard_map/ppermute | solution.py:412
  32.2 5.8 %collective-permute-start.6 = (f32[64,128]{1,0:T(8,128)S(1)}, f32[64,128]{1,0:T(8,128)S(1)}, u32[]{:S(2)}, u32[]{:S(2)}) collective-permute-start(f32[64,128]{1,0:T(8,128)S(1)} %get-tuple-element.35.own_ref), channel_id=1, source_target_pairs={{0,24},{4,28},{8,16},{12,20},{16,8},{20,12},{24,0},{28,4},{32,56},... | collective-permute-start | bytes 98312 | tf_op jit(solution)/shard_map/ppermute | solution.py:412
  36.9 9.9 %collective-permute-start.13 = (f32[2,64,128]{2,1,0:T(8,128)S(1)}, f32[2,64,128]{2,1,0:T(8,128)S(1)}, u32[]{:S(2)}, u32[]{:S(2)}) collective-permute-start(f32[2,64,128]{2,1,0:T(8,128)S(1)} %get-tuple-element.44), channel_id=1, source_target_pairs={{0,1},{1,0},{2,3},{3,2},{4,5},{5,4},{6,7},{7,6},{8,9},{9,8},{10,11... | collective-permute-start | bytes 196616 | tf_op jit(solution)/shard_map/ppermute | solution.py:412
  37.0 9.8 %collective-permute-start.14 = (f32[2,64,128]{2,1,0:T(8,128)S(1)}, f32[2,64,128]{2,1,0:T(8,128)S(1)}, u32[]{:S(2)}, u32[]{:S(2)}) collective-permute-start(f32[2,64,128]{2,1,0:T(8,128)S(1)} %get-tuple-element.45), channel_id=1, source_target_pairs={{0,3},{1,2},{2,1},{3,0},{4,7},{5,6},{6,5},{7,4},{8,11},{9,10},{10,... | collective-permute-start | bytes 196616 | tf_op jit(solution)/shard_map/ppermute | solution.py:417
  38.0 6.3 %collective-permute-start.7 = (f32[64,128]{1,0:T(8,128)S(1)}, f32[64,128]{1,0:T(8,128)S(1)}, u32[]{:S(2)}, u32[]{:S(2)}) collective-permute-start(f32[64,128]{1,0:T(8,128)S(1)} %get-tuple-element.37), channel_id=1, source_target_pairs={{0,56},{4,60},{8,48},{12,52},{16,40},{20,44},{24,32},{28,36},{32,2... | collective-permute-start | bytes 98312 | tf_op jit(solution)/shard_map/ppermute | solution.py:412
  44.4 6.1 %collective-permute-start.8 = (f32[64,128]{1,0:T(8,128)S(1)}, f32[64,128]{1,0:T(8,128)S(1)}, u32[]{:S(2)}, u32[]{:S(2)}) collective-permute-start(f32[64,128]{1,0:T(8,128)S(1)} %shard_map.41.half_ref), channel_id=1, source_target_pairs={{0,4},{4,0},{8,12},{12,8},{16,20},{20,16},{24,28},{28,24},{32,36},... | collective-permute-start | bytes 98312 | tf_op jit(solution)/shard_map/ppermute | solution.py:412

commit v2 on v1

--- a/solution.py
+++ b/solution.py
@@ -190,80 +190,70 @@
     out_ref[...] = high_bit("gy", 3, got_ref, low_ref)
 
 
-def local_body(nb, v_ref, cz_ref, cx_ref, out_ref, acc):
-    i = pl.program_id(0)
-    ny, nz = acc.shape
+def local_body(nb, v_ref, cz_ref, cx_ref, out_ref):
+    nx, ny, nz = v_ref.shape
     up = upper(nz)
-
-    @pl.when(i == 0)
-    def _():
-        acc[...] = scan_rows(times(cx_ref[...], up))
-
     lane = iota((ny, nz), 1)
-    cz = cz_ref[...]
-    rows = []
-    for j in range(nb):
-        x = i * nb + j
-        rows.append(v_ref[j] + jnp.where(lane == 0, pltpu.roll(cz, lax.rem(nz - x, nz), 1), 0.0))
-    along = times(jnp.concatenate(rows, axis=0), up).reshape(nb, ny, nz)
-    total = acc[...]
-    for j in range(nb):
-        total = total + scan_rows(along[j])
-        out_ref[j] = total
-    acc[...] = total
+
+    def block(i, total):
+        cz = cz_ref[...]
+        rows = []
+        for j in range(nb):
+            x = i * nb + j
+            rows.append(v_ref[x] + jnp.where(lane == 0, pltpu.roll(cz, lax.rem(nz - x, nz), 1), 0.0))
+        along = times(jnp.concatenate(rows, axis=0), up).reshape(nb, ny, nz)
+        for j in range(nb):
+            total = total + scan_rows(along[j])
+            out_ref[i * nb + j] = total
+        return total
+
+    lax.fori_loop(0, nx // nb, block, scan_rows(times(cx_ref[...], up)))
 
 
 def local(v, cz, cx):
-    nx, ny, nz = v.shape
     nb = 32
-    return call(
-        functools.partial(local_body, nb),
-        [v.shape],
-        grid=(nx // nb,),
-        ins=[pl.BlockSpec((nb, ny, nz), lambda i: (i, 0, 0)), whole(cz.shape), whole(cx.shape)],
-        outs=[pl.BlockSpec((nb, ny, nz), lambda i: (i, 0, 0))],
-        scratch=[pltpu.VMEM((ny, nz), F32)],
-        flops=1 << 29,
-        moved=8 << 20,
-    )(v, cz, cx)[0]
-
-
-def last_body(pieces, scale, s_ref, half_ref, other_half_ref, partner_ref, out_ref, gy, made, sems):
+    return call(functools.partial(local_body, nb), [v.shape], flops=1 << 29, moved=8 << 20)(v, cz, cx)[0]
+
+
+def finish_body(pieces, own, scale, s_ref, half_ref, partner_ref, *refs):
+    out_ref, made, sems = refs[-3:]
     core = lax.rem(lax.axis_index("gy"), 2)
     n = half_ref.shape[0]
-    mine, other = half_ref[...], other_half_ref[...]
-    for k in range(2):
-        part = jnp.where(core == k, mine, other)
-        gy[k * n : (k + 1) * n] = part + jnp.where(core == 1, partner_ref[k * n : (k + 1) * n], 0.0)
-    n = made.shape[0] // pieces
-    copies = []
+    at = n * (core if own else 1 - core)
+    step = n // pieces
+
+    def copy(k):
+        rows = pl.ds(k * step, step)
+        return pltpu.make_async_copy(made.at[rows], out_ref.at[pl.ds(at + k * step, step)], sems.at[k])
+
     for k in range(pieces):
 
         def group(i, _):
-            rows = gy[pl.ds(pl.multiple_of(i * 8, 8), 8), :]
+            theirs = partner_ref[pl.ds(pl.multiple_of(at + i * 8, 8), 8), :]
+            rows = half_ref[pl.ds(pl.multiple_of(i * 8, 8), 8), :] + jnp.where(core == 1, theirs, 0.0)
             for j in range(8):
-                made[i * 8 + j] = (s_ref[i * 8 + j] + rows[j : j + 1]) * scale
+                made[i * 8 + j] = (s_ref[at + i * 8 + j] + rows[j : j + 1]) * scale
             return 0
 
-        lax.fori_loop(k * n // 8, (k + 1) * n // 8, group, 0)
-        copies.append(pltpu.make_async_copy(made.at[pl.ds(k * n, n)], out_ref.at[pl.ds(k * n, n)], sems.at[k]))
-        copies[k].start()
-    for copy in copies:
-        copy.wait()
-
-
-def last(s, half, other_half, partner, scale):
-    nx, _, nz = s.shape
+        lax.fori_loop(k * step // 8, (k + 1) * step // 8, group, 0)
+        copy(k).start()
+    for k in range(pieces):
+        copy(k).wait()
+
+
+def finish(s, half, partner, scale, *begun):
+    nx, ny, nz = s.shape
     pieces = 8
     return pl.pallas_call(
-        functools.partial(last_body, pieces, scale),
+        functools.partial(finish_body, pieces, not begun, scale),
         out_shape=jax.ShapeDtypeStruct(s.shape, F32),
-        in_specs=[pl.BlockSpec(memory_space=pltpu.VMEM)] * 4,
+        in_specs=[pl.BlockSpec(memory_space=pltpu.VMEM)] * 3 + [pl.BlockSpec(memory_space=pltpu.HBM)] * len(begun),
         out_specs=pl.BlockSpec(memory_space=pltpu.HBM),
-        scratch_shapes=[pltpu.VMEM((nx, nz), F32), pltpu.VMEM(s.shape, F32), pltpu.SemaphoreType.DMA((pieces,))],
+        scratch_shapes=[pltpu.VMEM((nx // 2, ny, nz), F32), pltpu.SemaphoreType.DMA((pieces,))],
+        input_output_aliases={3: 0} if begun else {},
         compiler_params=pltpu.CompilerParams(vmem_limit_bytes=24 * MIB),
-        cost_estimate=cost(1 << 24, 8 << 20),
-    )(s, half, other_half, partner)
+        cost_estimate=cost(1 << 23, 4 << 20),
+    )(s, half, partner, *begun)
 
 
 def sides(axis, near, far):
@@ -310,13 +300,13 @@
 
 
 def box_xy_body(nb, v_ref, x_near, x_far, y_near, y_far, out_ref, near_ref, far_ref):
-    i = pl.program_id(0)
-    steps = pl.num_programs(0)
     ny, nz = v_ref.shape[1:]
-    base = pl.multiple_of(i * nb, nb)
-    group = lax.div(i * nb * 2, nz)
-
-    def run(first, final):
+    steps = v_ref.shape[0] // nb
+
+    def run(i, first, final):
+        base = pl.multiple_of(i * nb, nb)
+        group = lax.div(i * nb * 2, nz)
+
         def row(j):
             if first and j < 0:
                 return sides("gx", x_near[j + 2], x_far[j + 2])[0]
@@ -336,7 +326,7 @@
                 [lows[0][j : j + 1], lows[1][j : j + 1], along, highs[0][j : j + 1], highs[1][j : j + 1]], axis=0
             )
             box = five_rows(ext)
-            out_ref[j] = box
+            out_ref[base + j] = box
             at = lax.rem(base + j, nz // 2) * 2
             here = lax.div(lane, 2) * 2 == at
             up = jnp.where(here, pltpu.roll(box, lax.rem(at + 2, nz), 1), up)
@@ -347,9 +337,13 @@
         near_ref[group] = jnp.where(mine, near, near_ref[group])
         far_ref[group] = jnp.where(mine, far, far_ref[group])
 
-    pl.when(i == 0)(lambda: run(True, False))
-    pl.when(i == steps - 1)(lambda: run(False, True))
-    pl.when(jnp.logical_and(i > 0, i < steps - 1))(lambda: run(False, False))
+    def inner(i, _):
+        run(i, False, False)
+        return 0
+
+    run(jnp.int32(0), True, False)
+    lax.fori_loop(1, steps - 1, inner, 0)
+    run(jnp.int32(steps - 1), False, True)
 
 
 def box_xy(v, x_near, x_far, y_near, y_far):
@@ -357,55 +351,62 @@
     nb = 32
     packed = (2 * nx // nz, ny, nz)
     return call(
-        functools.partial(box_xy_body, nb),
-        [v.shape, packed, packed],
-        grid=(nx // nb,),
-        ins=[whole(v.shape), whole(x_near.shape), whole(x_far.shape), whole(y_near.shape), whole(y_far.shape)],
-        outs=[pl.BlockSpec((nb, ny, nz), lambda i: (i, 0, 0)), whole(packed), whole(packed)],
-        flops=1 << 26,
-        moved=8 << 20,
+        functools.partial(box_xy_body, nb), [v.shape, packed, packed], flops=1 << 26, moved=8 << 20
     )(v, x_near, x_far, y_near, y_far)
 
 
-def box_z_body(nb, scale, w_ref, near_ref, far_ref, out_ref, both):
-    i = pl.program_id(0)
-    ny, nz = w_ref.shape[1:]
+def box_z_body(scale, w_ref, near_ref, far_ref, out_ref, both, made, sems):
+    nx, ny, nz = w_ref.shape
+    nb = nz // 4
     lane = iota((ny, nz), 1)
-
-    @pl.when(i == 0)
-    def _():
-        source, target = iota((nz, nz), 0), iota((nz, nz), 1)
-        even = lax.rem(lane, 2) == 0
-        for g in range(near_ref.shape[0]):
-            lo, hi = sides("gz", near_ref[g], far_ref[g])
-            lo = lo + jnp.where(even, pltpu.roll(lo, nz - 1, 1), 0.0)
-            hi = hi + jnp.where(even, 0.0, pltpu.roll(hi, 1, 1))
-            for k in range(2):
-                place = lax.div(source, 2) * 4 + lax.rem(source, 2) - k * nz
-                both[2 * g + k] = times(hi, ones_where(target == place)) + times(lo, ones_where(target == place + 2))
+    source, target = iota((nz, nz), 0), iota((nz, nz), 1)
+    even = lax.rem(lane, 2) == 0
+    for g in range(near_ref.shape[0]):
+        lo, hi = sides("gz", near_ref[g], far_ref[g])
+        lo = lo + jnp.where(even, pltpu.roll(lo, nz - 1, 1), 0.0)
+        hi = hi + jnp.where(even, 0.0, pltpu.roll(hi, 1, 1))
+        for k in range(2):
+            place = lax.div(source, 2) * 4 + lax.rem(source, 2) - k * nz
+            both[2 * g + k] = times(hi, ones_where(target == place)) + times(lo, ones_where(target == place + 2))
 
     away = iota((nz, nz), 0) - iota((nz, nz), 1)
     band = ones_where(jnp.logical_and(away <= 2, away >= -2))
-    along = times(w_ref[...].reshape(nb * ny, nz), band).reshape(nb, ny, nz)
     edge = jnp.logical_or(lane < 2, lane >= nz - 2)
-    side = both[i]
-    for j in range(nb):
-        out_ref[j] = (along[j] + jnp.where(edge, pltpu.roll(side, (2 * nz - 2 - 4 * j) % nz, 1), 0.0)) * scale
+
+    def copy(i):
+        at = pl.ds(i * nb, nb)
+        return pltpu.make_async_copy(made.at[at], out_ref.at[at], sems.at[i])
+
+    def block(i, _):
+        along = times(w_ref[pl.ds(i * nb, nb)].reshape(nb * ny, nz), band).reshape(nb, ny, nz)
+        side = both[i]
+        for j in range(nb):
+            lacking = jnp.where(edge, pltpu.roll(side, (2 * nz - 2 - 4 * j) % nz, 1), 0.0)
+            made[i * nb + j] = (along[j] + lacking) * scale
+        copy(i).start()
+        return 0
+
+    lax.fori_loop(0, nx // nb, block, 0)
+    for i in range(nx // nb):
+        copy(i).wait()
 
 
 def box_z(w, near, far, scale):
     nx, ny, nz = w.shape
-    nb = nz // 4
-    return call(
-        functools.partial(box_z_body, nb, scale),
-        [w.shape],
-        grid=(nx // nb,),
-        ins=[pl.BlockSpec((nb, ny, nz), lambda i: (i, 0, 0)), whole(near.shape), whole(far.shape)],
-        outs=[pl.BlockSpec((nb, ny, nz), lambda i: (i, 0, 0))],
-        scratch=[pltpu.VMEM((nx // nb, ny, nz), F32)],
-        flops=1 << 29,
-        moved=8 << 20,
-    )(w, near, far)[0]
+    steps = 4 * nx // nz
+    return pl.pallas_call(
+        functools.partial(box_z_body, scale),
+        out_shape=jax.ShapeDtypeStruct(w.shape, F32),
+        in_specs=[pl.BlockSpec(memory_space=pltpu.VMEM)] * 3,
+        out_specs=pl.BlockSpec(memory_space=pltpu.HBM),
+        scratch_shapes=[
+            pltpu.VMEM((steps, ny, nz), F32),
+            pltpu.VMEM(w.shape, F32),
+            pltpu.SemaphoreType.DMA((steps,)),
+        ],
+        compiler_params=pltpu.CompilerParams(vmem_limit_bytes=24 * MIB),
+        cost_estimate=cost(1 << 29, 8 << 20),
+    )(w, near, far)
 
 
 def swap(v, axis, mask):
@@ -424,9 +425,10 @@
     held, rx, ry, near, far = xy_totals(v)
 
     got = swap(rx, "gx", 1)
-    x_near, x_far = swap(near, "gx", 1), away(far, "gx")
+    x_far = away(far, "gx")
     low, own = merge("gx", 0, got, rx)
     got = swap(own, "gx", 3)
+    x_near = swap(near, "gx", 1)
     (rz,) = call(z_totals_body, [(ny, nx)])(held)
     (ry,) = call(spread_body, [ry.shape])(ry)
     cx, rz = call(after_x_body, [rx.shape, rz.shape])(got, low, rz)
@@ -451,7 +453,9 @@
     box_sum = box_z(w, z_near, z_far, 1.0 / math.sqrt(125.0))
     (low,) = call(after_y_body, [low.shape])(got, low)
     other_low = swap(low, "gy", 1)
-    prefix = last(s, low, other_low, other, 1.0 / math.sqrt(cells))
+    scale = 1.0 / math.sqrt(cells)
+    prefix = finish(s, low, other, scale)
+    prefix = finish(s, other_low, other, scale, prefix)
     return (prefix, box_sum)
 
 

time: 52.7 us -> 53.2 us (level)
  starting transfers between devices: 27.4 us -> 28.3 us
    ppermute x3, starting transfers between devices: 2.69 us -> 3.39 us  [away(): lax.ppermute(v, axis, [(i, (i + 2 * (i % 2) - 1) % n) for i in range(n)])]
    pallas_call x4 -> x5, Pallas kernels: 12.2 us -> 12.1 us  [the longest x1 3.33 us: local(): call(functools.partial(local_body, nb), [v.shape], flops=1 << 29, moved=8...]
  transfers between devices with their start and end apart: 15 -> 15, of which waited for: 4 -> 4; matrix products, arithmetic and copies ran while one was open for 0% -> 0% of each run, Pallas kernels for 25% -> 26%
where the time goes in v2:
time: 53.2 us; the launch traced here: 53.1 us
  starting transfers between devices  28.3 us (53%)
  Pallas kernels  17.6 us (33%)
  waiting for transfers between devices  6.46 us (12%)
  between operations  0.78 us (1%)
    ppermute x12, starting transfers between devices, swap(): lax.ppermute(v, axis, [(i, i ^ mask) for i in range(lax.axis_size(axis))])  24.9 us
    ppermute x12, waiting for transfers between devices, swap(): lax.ppermute(v, axis, [(i, i ^ mask) for i in range(lax.axis_size(axis))])  6.46 us
    ppermute x3, starting transfers between devices, away(): lax.ppermute(v, axis, [(i, (i + 2 * (i % 2) - 1) % n) for i in range(n)])  3.39 us
    pallas_call x1, Pallas kernels, local(): call(functools.partial(local_body, nb), [v.shape], flops=1 << 29, moved=8...  3.33 us
    pallas_call x1, Pallas kernels, box_z(): pl.pallas_call(functools.partial(box_z_body, scale), out_shape=jax.ShapeD...  3.1 us
    pallas_call x1, Pallas kernels, box_xy(): call(functools.partial(box_xy_body, nb), [v.shape, packed, packed], flops...  2.83 us
    pallas_call x2, Pallas kernels, finish(): pl.pallas_call(functools.partial(finish_body, pieces, not begun, scale),...  2.83 us
    pallas_call x1, Pallas kernels, xy_totals(): pl.pallas_call(functools.partial(xy_totals_body, pieces), out_shape=[jax....  2.3 us
  transfers between devices with their start and end apart: 15, of which 4 were waited for; matrix products, arithmetic and copies ran while one was open for 0% of the time, Pallas kernels for 26%

profile of v2, /device:TPU:1, one launch (start us, length us, event | category | flops | bytes accessed | tf_op | source)
XLA Modules:
  0.0 53.1 jit_solution(15199147326252249636)
XLA Ops:
  0.6 2.3 %shard_map.30 = (f32[128,64,128]{2,1,0:T(8,128)S(1)}, f32[64,128]{1,0:T(8,128)S(1)}, f32[128,128]{1,0:T(8,128)S(1)}, f32[2,64,128]{2,1,0:T(8,128)S(1)}, f32[2,64,128]{2,1,0:T(8,128)S(1)}) custom-call(f32[128,64,128]{2,1,0:T(8,128)} %v_ref.1), custom_call_target="tpu_custom_call" | custom-call | flops 6291456 | bytes 8388608 | tf_op jit(solution)/shard_map/pallas_call | solution.py:121
  2.9 2.1 %collective-permute-start = (f32[64,128]{1,0:T(8,128)S(1)}, f32[64,128]{1,0:T(8,128)S(1)}, u32[]{:S(2)}, u32[]{:S(2)}) collective-permute-start(f32[64,128]{1,0:T(8,128)S(1)} %get-tuple-element.25.own_ref), channel_id=1, source_target_pairs={{0,64},{64,0},{128,192},{192,128},{1,65},{65,1},{129,193},{193,129... | collective-permute-start | bytes 98312 | tf_op jit(solution)/shard_map/ppermute | solution.py:413
  5.0 1.3 %collective-permute-done.from_ref = f32[64,128]{1,0:T(8,128)S(1)} collective-permute-done((f32[64,128]{1,0:T(8,128)S(1)}, f32[64,128]{1,0:T(8,128)S(1)}, u32[]{:S(2)}, u32[]{:S(2)}) %collective-permute-start) | collective-permute-done | bytes 32800 | tf_op jit(solution)/shard_map/ppermute | solution.py:413
  6.4 2.8 %collective-permute-start.1 = (f32[64,128]{1,0:T(8,128)S(1)}, f32[64,128]{1,0:T(8,128)S(1)}, u32[]{:S(2)}, u32[]{:S(2)}) collective-permute-start(f32[64,128]{1,0:T(8,128)S(1)} %get-tuple-element.26), channel_id=1, source_target_pairs={{0,192},{64,128},{128,64},{192,0},{1,193},{65,129},{129,65},{193,1... | collective-permute-start | bytes 98312 | tf_op jit(solution)/shard_map/ppermute | solution.py:413
  9.2 0.0 collective-permute-start.9
  9.2 0.8 %collective-permute-start.10 = (f32[2,64,128]{2,1,0:T(8,128)S(1)}, f32[2,64,128]{2,1,0:T(8,128)S(1)}, u32[]{:S(2)}, u32[]{:S(2)}) collective-permute-start(f32[2,64,128]{2,1,0:T(8,128)S(1)} %get-tuple-element.40), channel_id=1, source_target_pairs={{0,192},{64,128},{128,64},{192,0},{1,193},{65,129},{129,65},{193,1... | collective-permute-start | bytes 196616 | tf_op jit(solution)/shard_map/ppermute | solution.py:418
  10.0 2.3 %shard_map.32.rz_ref = f32[64,128]{1,0:T(8,128)S(1)} custom-call(f32[128,64,128]{2,1,0:T(8,128)S(1)} %get-tuple-element.24.v_ref.first_ref.last_ref), custom_call_target="tpu_custom_call" | custom-call | flops 1048576 | bytes 1048576 | tf_op jit(solution)/shard_map/pallas_call | solution.py:432
  12.3 0.0 collective-permute-done.1.got_ref
  12.3 0.1 shard_map.33
  12.4 1.3 %collective-permute-start.2 = (f32[64,128]{1,0:T(8,128)S(1)}, f32[64,128]{1,0:T(8,128)S(1)}, u32[]{:S(2)}, u32[]{:S(2)}) collective-permute-start(f32[64,128]{1,0:T(8,128)S(1)} %get-tuple-element.28.own_ref), channel_id=1, source_target_pairs={{0,1},{1,0},{2,3},{3,2},{4,5},{5,4},{6,7},{7,6},{8,9},{9,8},{10,11... | collective-permute-start | bytes 98312 | tf_op jit(solution)/shard_map/ppermute | solution.py:413
  13.7 1.5 %collective-permute-done.2.from_ref = f32[64,128]{1,0:T(8,128)S(1)} collective-permute-done((f32[64,128]{1,0:T(8,128)S(1)}, f32[64,128]{1,0:T(8,128)S(1)}, u32[]{:S(2)}, u32[]{:S(2)}) %collective-permute-start.2) | collective-permute-done | bytes 32800 | tf_op jit(solution)/shard_map/ppermute | solution.py:413
  15.2 2.8 %collective-permute-start.3 = (f32[64,128]{1,0:T(8,128)S(1)}, f32[64,128]{1,0:T(8,128)S(1)}, u32[]{:S(2)}, u32[]{:S(2)}) collective-permute-start(f32[64,128]{1,0:T(8,128)S(1)} %get-tuple-element.29), channel_id=1, source_target_pairs={{0,3},{1,2},{2,1},{3,0},{4,7},{5,6},{6,5},{7,4},{8,11},{9,10},{10,... | collective-permute-start | bytes 98312 | tf_op jit(solution)/shard_map/ppermute | solution.py:413
  18.0 0.0 collective-permute-done.9.near_a.near_b.x_near
  18.0 0.0 collective-permute-done.10.far_a.far_b.x_far
  18.0 0.3 shard_map.44
  18.3 4.2 %collective-permute-start.11 = (f32[2,128,128]{2,1,0:T(8,128)S(1)}, f32[2,128,128]{2,1,0:T(8,128)S(1)}, u32[]{:S(2)}, u32[]{:S(2)}) collective-permute-start(f32[2,128,128]{2,1,0:T(8,128)S(1)} %get-tuple-element.41), channel_id=1, source_target_pairs={{0,4},{4,0},{8,12},{12,8},{16,20},{20,16},{24,28},{28,24},{32,36},... | collective-permute-start | bytes 393224 | tf_op jit(solution)/shard_map/ppermute | solution.py:413
  22.5 1.6 %collective-permute-start.12 = (f32[2,128,128]{2,1,0:T(8,128)S(1)}, f32[2,128,128]{2,1,0:T(8,128)S(1)}, u32[]{:S(2)}, u32[]{:S(2)}) collective-permute-start(f32[2,128,128]{2,1,0:T(8,128)S(1)} %get-tuple-element.42), channel_id=1, source_target_pairs={{0,60},{4,8},{8,4},{12,16},{16,12},{20,24},{24,20},{28,32},{32,28}... | collective-permute-start | bytes 393224 | tf_op jit(solution)/shard_map/ppermute | solution.py:418
  24.1 0.3 shard_map.35.ry_ref
  24.5 0.0 collective-permute-done.3.got_ref
  24.5 0.1 shard_map.36
  24.6 4.4 %collective-permute-start.4 = (f32[128,128]{1,0:T(8,128)S(1)}, f32[128,128]{1,0:T(8,128)S(1)}, u32[]{:S(2)}, u32[]{:S(2)}) collective-permute-start(f32[128,128]{1,0:T(8,128)S(1)} %get-tuple-element.34.mine_ref), channel_id=1, source_target_pairs={{0,4},{4,0},{8,12},{12,8},{16,20},{20,16},{24,28},{28,24},{32,36},... | collective-permute-start | bytes 196616 | tf_op jit(solution)/shard_map/ppermute | solution.py:413
  29.0 0.9 %collective-permute-done.4.other_ref.partner_ref = f32[128,128]{1,0:T(8,128)S(1)} collective-permute-done((f32[128,128]{1,0:T(8,128)S(1)}, f32[128,128]{1,0:T(8,128)S(1)}, u32[]{:S(2)}, u32[]{:S(2)}) %collective-permute-start.4) | collective-permute-done | bytes 65568 | tf_op jit(solution)/shard_map/ppermute | solution.py:413
  30.0 0.1 collective-permute-start.5
  30.1 2.8 %collective-permute-done.5.from_ref = f32[64,128]{1,0:T(8,128)S(1)} collective-permute-done((f32[64,128]{1,0:T(8,128)S(1)}, f32[64,128]{1,0:T(8,128)S(1)}, u32[]{:S(2)}, u32[]{:S(2)}) %collective-permute-start.5) | collective-permute-done | bytes 32800 | tf_op jit(solution)/shard_map/ppermute | solution.py:413
  32.8 1.6 %collective-permute-start.6 = (f32[64,128]{1,0:T(8,128)S(1)}, f32[64,128]{1,0:T(8,128)S(1)}, u32[]{:S(2)}, u32[]{:S(2)}) collective-permute-start(f32[64,128]{1,0:T(8,128)S(1)} %get-tuple-element.35.own_ref), channel_id=1, source_target_pairs={{0,24},{4,28},{8,16},{12,20},{16,8},{20,12},{24,0},{28,4},{32,56},... | collective-permute-start | bytes 98312 | tf_op jit(solution)/shard_map/ppermute | solution.py:413
  34.5 0.0 collective-permute-done.11.y_near
  34.5 0.0 collective-permute-done.12.y_far
  34.5 2.8 %shard_map.45 = (f32[128,64,128]{2,1,0:T(8,128)S(1)}, f32[2,64,128]{2,1,0:T(8,128)S(1)}, f32[2,64,128]{2,1,0:T(8,128)S(1)}) custom-call(f32[128,64,128]{2,1,0:T(8,128)S(1)} %get-tuple-element.24.v_ref.first_ref.last_ref, f32[2,64,128]{2,1,0:T(8,128)S(1)} %collective-permute-done.9.near_a.near_b.x_near, ...), custom_call_target="tpu_custom_call" | custom-call | flops 67108864 | bytes 8388608 | tf_op jit(solution)/shard_map/pallas_call | solution.py:353
  37.3 0.1 collective-permute-start.13
  37.4 1.0 %collective-permute-start.14 = (f32[2,64,128]{2,1,0:T(8,128)S(1)}, f32[2,64,128]{2,1,0:T(8,128)S(1)}, u32[]{:S(2)}, u32[]{:S(2)}) collective-permute-start(f32[2,64,128]{2,1,0:T(8,128)S(1)} %get-tuple-element.45), channel_id=1, source_target_pairs={{0,3},{1,2},{2,1},{3,0},{4,7},{5,6},{6,5},{7,4},{8,11},{9,10},{10,... | collective-permute-start | bytes 196616 | tf_op jit(solution)/shard_map/ppermute | solution.py:418
  38.4 0.0 collective-permute-done.6.from_ref
  38.4 2.9 %collective-permute-start.7 = (f32[64,128]{1,0:T(8,128)S(1)}, f32[64,128]{1,0:T(8,128)S(1)}, u32[]{:S(2)}, u32[]{:S(2)}) collective-permute-start(f32[64,128]{1,0:T(8,128)S(1)} %get-tuple-element.37), channel_id=1, source_target_pairs={{0,56},{4,60},{8,48},{12,52},{16,40},{20,44},{24,32},{28,36},{32,2... | collective-permute-start | bytes 98312 | tf_op jit(solution)/shard_map/ppermute | solution.py:413
  41.3 3.3 %shard_map.37.s_ref = f32[128,64,128]{2,1,0:T(8,128)S(1)} custom-call(f32[128,64,128]{2,1,0:T(8,128)S(1)} %get-tuple-element.24.v_ref.first_ref.last_ref, f32[64,128]{1,0:T(8,128)S(1)} %get-tuple-element.33.cz_ref, f32[64,128]{1,0:T(8,128)S(1)} %get-tuple-element.31.cx_ref), custom_call_target="tpu_custom_call" | custom-call | flops 536870912 | bytes 8388608 | tf_op jit(solution)/shard_map/pallas_call | solution.py:215
  44.7 0.0 collective-permute-done.7.got_ref
  44.7 2.4 %collective-permute-start.8 = (f32[64,128]{1,0:T(8,128)S(1)}, f32[64,128]{1,0:T(8,128)S(1)}, u32[]{:S(2)}, u32[]{:S(2)}) collective-permute-start(f32[64,128]{1,0:T(8,128)S(1)} %shard_map.41.half_ref), channel_id=1, source_target_pairs={{0,4},{4,0},{8,12},{12,8},{16,20},{20,16},{24,28},{28,24},{32,36},... | collective-permute-start | bytes 98312 | tf_op jit(solution)/shard_map/ppermute | solution.py:413
  47.1 0.0 collective-permute-done.13.near_ref
  47.1 0.0 collective-permute-done.14.far_ref
  47.1 3.1 %shard_map.46 = f32[128,64,128]{2,1,0:T(8,128)} custom-call(f32[128,64,128]{2,1,0:T(8,128)S(1)} %get-tuple-element.43.w_ref, f32[2,64,128]{2,1,0:T(8,128)S(1)} %collective-permute-done.13.near_ref, f32[2,64,128]{2,1,0:T(8,128)S(1)} %collective-permute-done.14.far_ref), custom_call_target="tpu_custom_call" | custom-call | flops 536870912 | bytes 8388608 | tf_op jit(solution)/shard_map/pallas_call | solution.py:397
  50.3 1.4 %shard_map.42.refs_0_ = f32[128,64,128]{2,1,0:T(8,128)} custom-call(f32[128,64,128]{2,1,0:T(8,128)S(1)} %shard_map.37.s_ref, f32[64,128]{1,0:T(8,128)S(1)} %shard_map.41.half_ref, f32[128,128]{1,0:T(8,128)S(1)} %collective-permute-done.4.other_ref.partner_ref), custom_call_target="tpu_custom_call" | custom-call | flops 8388608 | bytes 4194304 | tf_op jit(solution)/shard_map/pallas_call | solution.py:247
  51.7 0.0 collective-permute-done.8.half_ref
  51.7 1.4 %shard_map.43 = f32[128,64,128]{2,1,0:T(8,128)} custom-call(f32[128,64,128]{2,1,0:T(8,128)S(1)} %shard_map.37.s_ref, f32[64,128]{1,0:T(8,128)S(1)} %collective-permute-done.8.half_ref, f32[128,128]{1,0:T(8,128)S(1)} %collective-permute-done.4.other_ref.partner_ref, f32[128,64,128]{2,1,0:T(8,128)} %shard_map.42.refs_0_), custom_call_target="tpu_custom_call", output_to_operand_aliasing={{}: (3, {})} | custom-call | flops 8388608 | bytes 4194304 | tf_op jit(solution)/shard_map/pallas_call | solution.py:247
  (6 shorter events, 0.1 us)
Async XLA Ops:
  2.9 3.4 %collective-permute-start = (f32[64,128]{1,0:T(8,128)S(1)}, f32[64,128]{1,0:T(8,128)S(1)}, u32[]{:S(2)}, u32[]{:S(2)}) collective-permute-start(f32[64,128]{1,0:T(8,128)S(1)} %get-tuple-element.25.own_ref), channel_id=1, source_target_pairs={{0,64},{64,0},{128,192},{192,128},{1,65},{65,1},{129,193},{193,129... | collective-permute-start | bytes 98312 | tf_op jit(solution)/shard_map/ppermute | solution.py:413
  6.4 5.9 %collective-permute-start.1 = (f32[64,128]{1,0:T(8,128)S(1)}, f32[64,128]{1,0:T(8,128)S(1)}, u32[]{:S(2)}, u32[]{:S(2)}) collective-permute-start(f32[64,128]{1,0:T(8,128)S(1)} %get-tuple-element.26), channel_id=1, source_target_pairs={{0,192},{64,128},{128,64},{192,0},{1,193},{65,129},{129,65},{193,1... | collective-permute-start | bytes 98312 | tf_op jit(solution)/shard_map/ppermute | solution.py:413
  9.2 8.8 %collective-permute-start.9 = (f32[2,64,128]{2,1,0:T(8,128)S(1)}, f32[2,64,128]{2,1,0:T(8,128)S(1)}, u32[]{:S(2)}, u32[]{:S(2)}) collective-permute-start(f32[2,64,128]{2,1,0:T(8,128)S(1)} %get-tuple-element.39), channel_id=1, source_target_pairs={{0,64},{64,0},{128,192},{192,128},{1,65},{65,1},{129,193},{193,129... | collective-permute-start | bytes 196616 | tf_op jit(solution)/shard_map/ppermute | solution.py:413
  9.2 8.8 %collective-permute-start.10 = (f32[2,64,128]{2,1,0:T(8,128)S(1)}, f32[2,64,128]{2,1,0:T(8,128)S(1)}, u32[]{:S(2)}, u32[]{:S(2)}) collective-permute-start(f32[2,64,128]{2,1,0:T(8,128)S(1)} %get-tuple-element.40), channel_id=1, source_target_pairs={{0,192},{64,128},{128,64},{192,0},{1,193},{65,129},{129,65},{193,1... | collective-permute-start | bytes 196616 | tf_op jit(solution)/shard_map/ppermute | solution.py:418
  12.4 2.8 %collective-permute-start.2 = (f32[64,128]{1,0:T(8,128)S(1)}, f32[64,128]{1,0:T(8,128)S(1)}, u32[]{:S(2)}, u32[]{:S(2)}) collective-permute-start(f32[64,128]{1,0:T(8,128)S(1)} %get-tuple-element.28.own_ref), channel_id=1, source_target_pairs={{0,1},{1,0},{2,3},{3,2},{4,5},{5,4},{6,7},{7,6},{8,9},{9,8},{10,11... | collective-permute-start | bytes 98312 | tf_op jit(solution)/shard_map/ppermute | solution.py:413
  15.2 9.3 %collective-permute-start.3 = (f32[64,128]{1,0:T(8,128)S(1)}, f32[64,128]{1,0:T(8,128)S(1)}, u32[]{:S(2)}, u32[]{:S(2)}) collective-permute-start(f32[64,128]{1,0:T(8,128)S(1)} %get-tuple-element.29), channel_id=1, source_target_pairs={{0,3},{1,2},{2,1},{3,0},{4,7},{5,6},{6,5},{7,4},{8,11},{9,10},{10,... | collective-permute-start | bytes 98312 | tf_op jit(solution)/shard_map/ppermute | solution.py:413
  18.3 16.1 %collective-permute-start.11 = (f32[2,128,128]{2,1,0:T(8,128)S(1)}, f32[2,128,128]{2,1,0:T(8,128)S(1)}, u32[]{:S(2)}, u32[]{:S(2)}) collective-permute-start(f32[2,128,128]{2,1,0:T(8,128)S(1)} %get-tuple-element.41), channel_id=1, source_target_pairs={{0,4},{4,0},{8,12},{12,8},{16,20},{20,16},{24,28},{28,24},{32,36},... | collective-permute-start | bytes 393224 | tf_op jit(solution)/shard_map/ppermute | solution.py:413
  22.5 12.0 %collective-permute-start.12 = (f32[2,128,128]{2,1,0:T(8,128)S(1)}, f32[2,128,128]{2,1,0:T(8,128)S(1)}, u32[]{:S(2)}, u32[]{:S(2)}) collective-permute-start(f32[2,128,128]{2,1,0:T(8,128)S(1)} %get-tuple-element.42), channel_id=1, source_target_pairs={{0,60},{4,8},{8,4},{12,16},{16,12},{20,24},{24,20},{28,32},{32,28}... | collective-permute-start | bytes 393224 | tf_op jit(solution)/shard_map/ppermute | solution.py:418
  24.6 5.3 %collective-permute-start.4 = (f32[128,128]{1,0:T(8,128)S(1)}, f32[128,128]{1,0:T(8,128)S(1)}, u32[]{:S(2)}, u32[]{:S(2)}) collective-permute-start(f32[128,128]{1,0:T(8,128)S(1)} %get-tuple-element.34.mine_ref), channel_id=1, source_target_pairs={{0,4},{4,0},{8,12},{12,8},{16,20},{20,16},{24,28},{28,24},{32,36},... | collective-permute-start | bytes 196616 | tf_op jit(solution)/shard_map/ppermute | solution.py:413
  30.0 2.9 %collective-permute-start.5 = (f32[64,128]{1,0:T(8,128)S(1)}, f32[64,128]{1,0:T(8,128)S(1)}, u32[]{:S(2)}, u32[]{:S(2)}) collective-permute-start(f32[64,128]{1,0:T(8,128)S(1)} %shard_map.38.own_ref), channel_id=1, source_target_pairs={{0,8},{4,12},{8,0},{12,4},{16,24},{20,28},{24,16},{28,20},{32,40},... | collective-permute-start | bytes 98312 | tf_op jit(solution)/shard_map/ppermute | solution.py:413
  32.8 5.6 %collective-permute-start.6 = (f32[64,128]{1,0:T(8,128)S(1)}, f32[64,128]{1,0:T(8,128)S(1)}, u32[]{:S(2)}, u32[]{:S(2)}) collective-permute-start(f32[64,128]{1,0:T(8,128)S(1)} %get-tuple-element.35.own_ref), channel_id=1, source_target_pairs={{0,24},{4,28},{8,16},{12,20},{16,8},{20,12},{24,0},{28,4},{32,56},... | collective-permute-start | bytes 98312 | tf_op jit(solution)/shard_map/ppermute | solution.py:413
  37.3 9.8 %collective-permute-start.13 = (f32[2,64,128]{2,1,0:T(8,128)S(1)}, f32[2,64,128]{2,1,0:T(8,128)S(1)}, u32[]{:S(2)}, u32[]{:S(2)}) collective-permute-start(f32[2,64,128]{2,1,0:T(8,128)S(1)} %get-tuple-element.44), channel_id=1, source_target_pairs={{0,1},{1,0},{2,3},{3,2},{4,5},{5,4},{6,7},{7,6},{8,9},{9,8},{10,11... | collective-permute-start | bytes 196616 | tf_op jit(solution)/shard_map/ppermute | solution.py:413
  37.4 9.7 %collective-permute-start.14 = (f32[2,64,128]{2,1,0:T(8,128)S(1)}, f32[2,64,128]{2,1,0:T(8,128)S(1)}, u32[]{:S(2)}, u32[]{:S(2)}) collective-permute-start(f32[2,64,128]{2,1,0:T(8,128)S(1)} %get-tuple-element.45), channel_id=1, source_target_pairs={{0,3},{1,2},{2,1},{3,0},{4,7},{5,6},{6,5},{7,4},{8,11},{9,10},{10,... | collective-permute-start | bytes 196616 | tf_op jit(solution)/shard_map/ppermute | solution.py:418
  38.4 6.3 %collective-permute-start.7 = (f32[64,128]{1,0:T(8,128)S(1)}, f32[64,128]{1,0:T(8,128)S(1)}, u32[]{:S(2)}, u32[]{:S(2)}) collective-permute-start(f32[64,128]{1,0:T(8,128)S(1)} %get-tuple-element.37), channel_id=1, source_target_pairs={{0,56},{4,60},{8,48},{12,52},{16,40},{20,44},{24,32},{28,36},{32,2... | collective-permute-start | bytes 98312 | tf_op jit(solution)/shard_map/ppermute | solution.py:413
  44.7 7.0 %collective-permute-start.8 = (f32[64,128]{1,0:T(8,128)S(1)}, f32[64,128]{1,0:T(8,128)S(1)}, u32[]{:S(2)}, u32[]{:S(2)}) collective-permute-start(f32[64,128]{1,0:T(8,128)S(1)} %shard_map.41.half_ref), channel_id=1, source_target_pairs={{0,4},{4,0},{8,12},{12,8},{16,20},{20,16},{24,28},{28,24},{32,36},... | collective-permute-start | bytes 98312 | tf_op jit(solution)/shard_map/ppermute | solution.py:413
